TPU v7x, 128 devices: a whole 4x4x4 slice. The times are simulated.
128 devices in a mesh: expert: 4 (over x_lo, core), shard: 32 (over z, y, x_hi).
Axes of the slice: x: 4 (x_hi: 2, x_lo: 2; x = x_hi * 2 + x_lo), y: 4, z: 4, core: 2. Of those that a mesh axis runs over, the one named last changes fastest.
Arguments:
- master_gate: float32 [64, 2048, 1024], P('expert', 'shard'), may hold values from -0.25 to 0.25
- second_gate: bfloat16 [64, 2048, 1024], P('expert', 'shard'), may hold values from -0.0625 to 0.0625
- master_up: float32 [64, 2048, 1024], P('expert', 'shard'), may hold values from -0.25 to 0.25
- second_up: bfloat16 [64, 2048, 1024], P('expert', 'shard'), may hold values from -0.0625 to 0.0625
- master_down: float32 [64, 1024, 2048], P('expert', None, 'shard'), may hold values from -0.375 to 0.375
- second_down: bfloat16 [64, 1024, 2048], P('expert', None, 'shard'), may hold values from -0.09375 to 0.09375
- router_weight: float32 [2048, 64], P('shard', 'expert'), may hold values from -0.125 to 0.125
- router_gain: float32 [2048], P('shard'), may hold values from 0.25 to 1.75
Outputs:
- final_gate: bfloat16 [64, 2048, 1024], P('expert', None, 'shard')
- final_up: bfloat16 [64, 2048, 1024], P('expert', None, 'shard')
- final_down: bfloat16 [64, 1024, 2048], P('expert', 'shard')
- scale_gate: float32 [64, 1024], P('expert', 'shard')
- scale_up: float32 [64, 1024], P('expert', 'shard')
- scale_down: float32 [64, 1024], P('expert', 'shard')
- serve_router: bfloat16 [2048, 64], replicated
All inputs are finite; a program needn't handle non-finite values. Where the computation divides by a largest or mean magnitude, that divisor is 1e-20 or more.
Results may differ from a plain program's by a relative error of at most 0.001.
Values may be sent and summed in bfloat16 or wider, within the bound.
A program may use at most 128 MiB of HBM per device.

v0:
```python
import jax
import jax.numpy as jnp
from jax import lax
from jax.sharding import PartitionSpec as P


def over_pieces(array, axis):
    blocks = lax.all_gather(array, axis)
    return blocks.max(axis=0)


def joined_along(blocks, dim):
    blocks = jnp.moveaxis(blocks, 0, dim)
    lengths = blocks.shape
    return blocks.reshape(*lengths[:dim], lengths[dim] * lengths[dim + 1], *lengths[dim + 2 :])


def copy_for_each(array, axis):
    copies = jnp.broadcast_to(array, (lax.axis_size(axis), *array.shape))
    return lax.all_to_all(copies, axis, split_axis=0, concat_axis=0, tiled=True)


def gather_directly(array, axis, dim):
    return joined_along(copy_for_each(array, axis), dim)


def per_device(
    master_gate,
    second_gate,
    master_up,
    second_up,
    master_down,
    second_down,
    router_weight,
    router_gain,
):
    merged_gate = master_gate + second_gate.astype(jnp.float32)
    merged_up = master_up + second_up.astype(jnp.float32)
    merged_down = master_down + second_down.astype(jnp.float32)
    scale_gate, scale_up, scale_down = (
        over_pieces(jnp.max(jnp.abs(merged_gate), axis=1), "shard"),
        over_pieces(jnp.max(jnp.abs(merged_up), axis=1), "shard"),
        over_pieces(jnp.max(jnp.abs(merged_down), axis=2), "shard"),
    )
    narrow_gate, narrow_up, narrow_down = (
        (merged_gate / jnp.expand_dims(scale_gate, 1)).astype(jnp.bfloat16),
        (merged_up / jnp.expand_dims(scale_up, 1)).astype(jnp.bfloat16),
        (merged_down / jnp.expand_dims(scale_down, 2)).astype(jnp.bfloat16),
    )
    final_gate, final_up = (
        lax.all_to_all(narrow_gate, "shard", split_axis=2, concat_axis=1, tiled=True),
        lax.all_to_all(narrow_up, "shard", split_axis=2, concat_axis=1, tiled=True),
    )
    final_down = lax.all_to_all(narrow_down, "shard", split_axis=1, concat_axis=2, tiled=True)
    scale_gate = lax.dynamic_slice_in_dim(
        scale_gate, lax.axis_index("shard") * final_gate.shape[2], final_gate.shape[2], axis=1
    )
    scale_up = lax.dynamic_slice_in_dim(
        scale_up, lax.axis_index("shard") * final_up.shape[2], final_up.shape[2], axis=1
    )
    scale_down = lax.dynamic_slice_in_dim(
        scale_down, lax.axis_index("shard") * final_down.shape[1], final_down.shape[1], axis=1
    )
    part_router = (router_weight * router_gain[:, None]).astype(jnp.bfloat16)
    row_router = gather_directly(part_router, "shard", 0)
    serve_router = gather_directly(row_router, "expert", 1)
    return (final_gate, final_up, final_down, scale_gate, scale_up, scale_down, serve_router)


def solution(mesh):
    in_specs = (
        P("expert", "shard", None),
        P("expert", "shard", None),
        P("expert", "shard", None),
        P("expert", "shard", None),
        P("expert", None, "shard"),
        P("expert", None, "shard"),
        P("shard", "expert"),
        P("shard"),
    )
    out_specs = (
        P("expert", None, "shard"),
        P("expert", None, "shard"),
        P("expert", "shard", None),
        P("expert", "shard"),
        P("expert", "shard"),
        P("expert", "shard"),
        P(),
    )
    return jax.shard_map(
        per_device, mesh=mesh, in_specs=in_specs, out_specs=out_specs, check_vma=False
    )
```

profile of v0, /device:TPU:0, one launch (start us, length us, event | category | flops | bytes accessed | tf_op | source)
XLA Modules:
  0.0 351.2 jit_solution(11286700278686036596)
XLA Ops:
  16.2 10.9 %all-to-all-start.3 = ((bf16[32,2,512]{2,1,0:T(2,128)(2,1)}), bf16[32,2,512]{2,1,0:T(2,128)(2,1)S(1)}, u32[]{:S(2)}, u32[]{:S(2)}) async-start(bf16[32,2,512]{2,1,0:T(2,128)(2,1)} %reshape.35), calls=%async_computation.3 | async-start | bytes 131072 | tf_op jit(solution)/shard_map/all_to_all | solution.py:20
  31.5 5.4 %all-to-all-done.3 = bf16[32,2,512]{2,1,0:T(2,128)(2,1)S(1)} async-done(((bf16[32,2,512]{2,1,0:T(2,128)(2,1)}), bf16[32,2,512]{2,1,0:T(2,128)(2,1)S(1)}, u32[]{:S(2)}, u32[]{:S(2)}) %all-to-all-start.3) | async-done | bytes 65568 | tf_op jit(solution)/shard_map/all_to_all | solution.py:20
  41.4 43.4 %all-gather.7.cloned.1.call-done = f32[512,1024]{1,0:T(8,128)} async-done(((f32[16,1024]{1,0:T(8,128)}), f32[512,1024]{1,0:T(8,128)}) %all-gather.7.cloned.1.call-update) | async-done | bytes 2097168 | tf_op jit(solution)/shard_map/all_gather | solution.py:8
  90.9 6.2 %copy.120 = bf16[16,64,1024]{1,0,2:T(8,128)(2,1)} copy(bf16[16,64,1024]{2,1,0:T(8,128)(2,1)} %divide_convert_fusion.2) | data formatting | bytes 4194304 | tf_op jit(solution)/shard_map/convert_element_type | solution.py:46
  97.1 7.9 %reshape.29 = bf16[32,2,16384]{2,1,0:T(2,128)(2,1)} reshape(bf16[1024,16,64]{2,1,0:T(8,128)(2,1)} %bitcast.36) | data formatting | bytes 4194304
  105.0 5.9 %all-to-all-start = ((bf16[32,2,16384]{2,1,0:T(2,128)(2,1)}), bf16[32,2,16384]{2,1,0:T(2,128)(2,1)S(1)}, u32[]{:S(2)}, u32[]{:S(2)}) async-start(bf16[32,2,16384]{2,1,0:T(2,128)(2,1)} %reshape.29), calls=%async_computation | async-start | bytes 4194304 | tf_op jit(solution)/shard_map/all_to_all | solution.py:51
  110.8 58.5 %all-gather.9.cloned.1.call-done = f32[512,1024]{1,0:T(8,128)} async-done(((f32[16,1024]{1,0:T(8,128)}), f32[512,1024]{1,0:T(8,128)}) %all-gather.9.cloned.1.call-update) | async-done | bytes 2097168 | tf_op jit(solution)/shard_map/all_gather | solution.py:8
  171.1 5.0 %divide_convert_fusion.1 = bf16[16,64,1024]{2,1,0:T(8,128)(2,1)} fusion(f32[16,64,1024]{2,1,0:T(8,128)} %param.10, bf16[16,64,1024]{2,1,0:T(8,128)(2,1)} %param.11, f32[16,1024]{1,0:T(8,128)S(1)} %reduce_max.57), kind=kLoop, calls=%fused_computation.3 | loop fusion | flops 4194304 | bytes 8454144 | tf_op jit(solution)/shard_map/convert_element_type | solution.py:47
  176.1 6.2 %copy.125 = bf16[16,64,1024]{1,0,2:T(8,128)(2,1)} copy(bf16[16,64,1024]{2,1,0:T(8,128)(2,1)} %divide_convert_fusion.1) | data formatting | bytes 4194304 | tf_op jit(solution)/shard_map/convert_element_type | solution.py:47
  182.3 7.9 %reshape.31 = bf16[32,2,16384]{2,1,0:T(2,128)(2,1)} reshape(bf16[1024,16,64]{2,1,0:T(8,128)(2,1)} %bitcast.37) | data formatting | bytes 4194304
  190.1 6.2 %all-to-all-start.1 = ((bf16[32,2,16384]{2,1,0:T(2,128)(2,1)}), bf16[32,2,16384]{2,1,0:T(2,128)(2,1)}, u32[]{:S(2)}, u32[]{:S(2)}) async-start(bf16[32,2,16384]{2,1,0:T(2,128)(2,1)} %reshape.31), calls=%async_computation.1 | async-start | bytes 4194304 | tf_op jit(solution)/shard_map/all_to_all | solution.py:52
  196.3 58.2 %all-gather.11.cloned.1.call-done = f32[512,1024]{1,0:T(8,128)} async-done(((f32[16,1024]{1,0:T(8,128)}), f32[512,1024]{1,0:T(8,128)}) %all-gather.11.cloned.1.call-update) | async-done | bytes 2097168 | tf_op jit(solution)/shard_map/all_gather | solution.py:8
  256.2 5.0 %divide_convert_fusion = bf16[16,1024,64]{1,2,0:T(8,128)(2,1)} fusion(f32[16,1024,64]{1,2,0:T(8,128)} %param.12, bf16[16,1024,64]{1,2,0:T(8,128)(2,1)} %param.13, f32[16,1024]{1,0:T(8,128)S(1)} %reduce_max.59), kind=kLoop, calls=%fused_computation | loop fusion | flops 4194304 | bytes 8454144 | tf_op jit(solution)/shard_map/convert_element_type | solution.py:48
  261.2 6.2 %copy.130 = bf16[16,1024,64]{2,0,1:T(8,128)(2,1)} copy(bf16[16,1024,64]{1,2,0:T(8,128)(2,1)} %divide_convert_fusion) | data formatting | bytes 4194304 | tf_op jit(solution)/shard_map/convert_element_type | solution.py:48
  267.4 7.9 %reshape.33 = bf16[32,2,16384]{2,1,0:T(2,128)(2,1)} reshape(bf16[1024,16,64]{2,1,0:T(8,128)(2,1)} %bitcast.38) | data formatting | bytes 4194304
  275.3 6.0 %all-to-all-start.2 = ((bf16[32,2,16384]{2,1,0:T(2,128)(2,1)}), bf16[32,2,16384]{2,1,0:T(2,128)(2,1)}, u32[]{:S(2)}, u32[]{:S(2)}) async-start(bf16[32,2,16384]{2,1,0:T(2,128)(2,1)} %reshape.33), calls=%async_computation.2 | async-start | bytes 4194304 | tf_op jit(solution)/shard_map/all_to_all | solution.py:54
  287.3 6.9 %copy.122 = bf16[16,32,64,32]{2,1,3,0:T(8,128)(2,1)} copy(bf16[16,32,64,32]{2,0,3,1:T(8,128)(2,1)} %bitcast.39) | data formatting | bytes 4194304 | tf_op jit(solution)/shard_map/all_to_all | solution.py:51
  294.2 6.7 %all_to_all.48 = bf16[16,2048,32]{1,2,0:T(8,128)(2,1)} reshape(bf16[16,32,64,32]{2,1,3,0:T(8,128)(2,1)} %copy.122) | data formatting | bytes 4194304 | tf_op jit(solution)/shard_map/all_to_all | solution.py:51
  300.9 7.9 %reshape.32 = bf16[1024,16,64]{2,1,0:T(8,128)(2,1)} reshape(bf16[32,2,16384]{2,1,0:T(2,128)(2,1)} %all-to-all-done.1) | data formatting | bytes 4194304
  308.8 6.9 %copy.127 = bf16[16,32,64,32]{2,1,3,0:T(8,128)(2,1)} copy(bf16[16,32,64,32]{2,0,3,1:T(8,128)(2,1)} %bitcast.40) | data formatting | bytes 4194304 | tf_op jit(solution)/shard_map/all_to_all | solution.py:52
  315.7 6.7 %all_to_all.52 = bf16[16,2048,32]{1,2,0:T(8,128)(2,1)} reshape(bf16[16,32,64,32]{2,1,3,0:T(8,128)(2,1)} %copy.127) | data formatting | bytes 4194304 | tf_op jit(solution)/shard_map/all_to_all | solution.py:52
  322.5 7.9 %reshape.34 = bf16[1024,16,64]{2,1,0:T(8,128)(2,1)} reshape(bf16[32,2,16384]{2,1,0:T(2,128)(2,1)} %all-to-all-done.2) | data formatting | bytes 4194304
  330.4 6.9 %copy.132 = bf16[16,32,32,64]{3,2,1,0:T(8,128)(2,1)} copy(bf16[16,32,32,64]{3,0,1,2:T(8,128)(2,1)} %bitcast.41) | data formatting | bytes 4194304 | tf_op jit(solution)/shard_map/all_to_all | solution.py:54
  337.2 6.7 %all_to_all.56 = bf16[16,32,2048]{2,1,0:T(8,128)(2,1)} reshape(bf16[16,32,32,64]{3,2,1,0:T(8,128)(2,1)} %copy.132) | data formatting | bytes 4194304 | tf_op jit(solution)/shard_map/all_to_all | solution.py:54
  (38 shorter events, 34.1 us)
Async XLA Ops:
  7.2 4.5 %copy-start.1 = (bf16[16,64,1024]{2,1,0:T(8,128)(2,1)S(1)}, bf16[16,64,1024]{2,1,0:T(8,128)(2,1)}, u32[]{:S(2)}) copy-start(bf16[16,64,1024]{2,1,0:T(8,128)(2,1)} %param.11) | copy-start | bytes 6291460
  7.2 77.6 %all-gather.7.cloned.1.call-start = ((), (), s32[]{:S(2)}) async-start(), calls=%async_computation.5 | async-start | bytes 2162688 | tf_op jit(solution)/shard_map/all_gather | solution.py:8
  11.6 3.7 %copy-start.2 = (f32[64,16]{0,1:T(8,128)S(1)}, f32[64,16]{0,1:T(8,128)}, u32[]{:S(2)}) copy-start(f32[64,16]{0,1:T(8,128)} %param.14) | copy-start | bytes 12292
  11.6 3.7 %copy-start.3 = (f32[64]{0:T(128)S(1)}, f32[64]{0:T(128)}, u32[]{:S(2)}) copy-start(f32[64]{0:T(128)} %param.15) | copy-start | bytes 772
  11.7 157.7 %all-gather.9.cloned.1.call-start = ((), (), s32[]{:S(2)}) async-start(), calls=%async_computation.6 | async-start | bytes 2162688 | tf_op jit(solution)/shard_map/all_gather | solution.py:8
  16.2 20.8 %all-to-all-start.3 = ((bf16[32,2,512]{2,1,0:T(2,128)(2,1)}), bf16[32,2,512]{2,1,0:T(2,128)(2,1)S(1)}, u32[]{:S(2)}, u32[]{:S(2)}) async-start(bf16[32,2,512]{2,1,0:T(2,128)(2,1)} %reshape.35), calls=%async_computation.3 | async-start | bytes 131072 | tf_op jit(solution)/shard_map/all_to_all | solution.py:20
  27.1 59.5 %copy-start = (bf16[16,64,1024]{2,1,0:T(8,128)(2,1)S(1)}, bf16[16,64,1024]{2,1,0:T(8,128)(2,1)}, u32[]{:S(2)}) copy-start(bf16[16,64,1024]{2,1,0:T(8,128)(2,1)} %param.9) | copy-start | bytes 6291460
  27.1 227.5 %all-gather.11.cloned.1.call-start = ((), (), s32[]{:S(2)}) async-start(), calls=%async_computation.7 | async-start | bytes 2162688 | tf_op jit(solution)/shard_map/all_gather | solution.py:8
  38.0 66.9 %all-to-all-start.4 = ((bf16[4,2048,16]{1,2,0:T(8,128)(2,1)}), bf16[4,2048,16]{1,2,0:T(8,128)(2,1)S(1)}, u32[]{:S(2)}, u32[]{:S(2)}) async-start(bf16[4,2048,16]{1,2,0:T(8,128)(2,1)} %broadcast_in_dim.5), calls=%async_computation.4 | async-start | bytes 524288 | tf_op jit(solution)/shard_map/all_to_all | solution.py:20
  105.0 85.2 %all-to-all-start = ((bf16[32,2,16384]{2,1,0:T(2,128)(2,1)}), bf16[32,2,16384]{2,1,0:T(2,128)(2,1)S(1)}, u32[]{:S(2)}, u32[]{:S(2)}) async-start(bf16[32,2,16384]{2,1,0:T(2,128)(2,1)} %reshape.29), calls=%async_computation | async-start | bytes 4194304 | tf_op jit(solution)/shard_map/all_to_all | solution.py:51
  190.1 85.2 %all-to-all-start.1 = ((bf16[32,2,16384]{2,1,0:T(2,128)(2,1)}), bf16[32,2,16384]{2,1,0:T(2,128)(2,1)}, u32[]{:S(2)}, u32[]{:S(2)}) async-start(bf16[32,2,16384]{2,1,0:T(2,128)(2,1)} %reshape.31), calls=%async_computation.1 | async-start | bytes 4194304 | tf_op jit(solution)/shard_map/all_to_all | solution.py:52
  275.3 47.2 %all-to-all-start.2 = ((bf16[32,2,16384]{2,1,0:T(2,128)(2,1)}), bf16[32,2,16384]{2,1,0:T(2,128)(2,1)}, u32[]{:S(2)}, u32[]{:S(2)}) async-start(bf16[32,2,16384]{2,1,0:T(2,128)(2,1)} %reshape.33), calls=%async_computation.2 | async-start | bytes 4194304 | tf_op jit(solution)/shard_map/all_to_all | solution.py:54
Sparse Core Ops, SparseCore 0:
  11.8 73.0 all-gather.6
  88.5 80.8 all-gather.8
  173.0 81.4 all-gather.10
where the time goes:
time: 354 us; the launch traced here: 351 us
  waiting for transfers between devices  166 us (47%)
  local copies, waits for them, and re-layouts  107 us (30%)
  starting transfers between devices  32.4 us (9%)
  other arithmetic  31.9 us (9%)
  between operations  13.9 us (4%)
    all_gather x3, waiting for transfers between devices, over_pieces(): blocks = lax.all_gather(array, axis)  160 us
    unnamed x18, local copies, waits for them, and re-layouts  45.1 us
    all_to_all x2, starting transfers between devices, copy_for_each(): return lax.all_to_all(copies, axis, split_axis=0, concat_axis=0, tiled=True)  14.3 us
    all_to_all x2, local copies, waits for them, and re-layouts, per_device(): lax.all_to_all(narrow_up, 'shard', split_axis=2, concat_axis=1, tiled=True)  13.6 us
    all_to_all x2, local copies, waits for them, and re-layouts, per_device(): lax.all_to_all(narrow_gate, 'shard', split_axis=2, concat_axis=1, tiled=T...  13.6 us
    all_to_all x2, local copies, waits for them, and re-layouts, per_device(): lax.all_to_all(narrow_down, 'shard', split_axis=1, concat_axis=2, tiled=T...  13.6 us
  transfers between devices with their start and end apart: 8, of which 4 were waited for; matrix products, arithmetic and copies ran while one was open for 28% of the time, Pallas kernels for 0%

commit v1 on v0

v1 whole, which is shorter than its diff:
```python
import jax
import jax.numpy as jnp
from jax import lax
from jax.experimental import pallas as pl
from jax.experimental.pallas import tpu as pltpu
from jax.sharding import PartitionSpec as P

MESH = pl.DeviceIdType.MESH
F32, BF16 = jnp.float32, jnp.bfloat16
N = 32
E, R, C = 16, 64, 1024
W = C // N
GE = 4
NG = E // GE
OFFSETS = [
    (dx, dy, dz) for dx in range(2) for dy in range(4) for dz in range(4) if (dx, dy, dz) != (0, 0, 0)
]


def kernel(
    mg, sg, mu, su, md, sd, rw, rg,
    og, ou, od, cg, cu, cd, orr,
    mbuf, sbuf, lmax, rs_s, rs_r, ag_s, ag_r, inv, snd, rcv, rt_s, rt_r, rt_x,
    load_sem, rs_ss, rs_rs, ag_ss, ag_rs, d_ss, d_rs, rt_ss, rt_rs, rx_ss, rx_rs,
):
    e_id = lax.axis_index("expert")
    me = lax.axis_index("shard")
    xhi = lax.rem(me, 2)
    y = lax.rem(me // 2, 4)
    z = me // 8

    masters, seconds = (mg, mu, md), (sg, su, sd)
    for m in range(3):
        for g in range(NG):
            es = pl.ds(g * GE, GE)
            pltpu.make_async_copy(masters[m].at[es], mbuf.at[m, es], load_sem.at[0, m * NG + g]).start()
            pltpu.make_async_copy(seconds[m].at[es], sbuf.at[m, es], load_sem.at[1, m * NG + g]).start()

    peers = []
    for dx, dy, dz in OFFSETS:
        peers.append((lax.rem(z + dz, 4) * 4 + lax.rem(y + dy, 4)) * 2 + lax.rem(xhi + dx, 2))
    mates = [lax.rem(e_id + k, 4) for k in range(1, 4)]

    barrier = pltpu.get_barrier_semaphore()
    for p in peers:
        pl.semaphore_signal(barrier, inc=1, device_id=(e_id, p), device_id_type=MESH)
    for q in mates:
        pl.semaphore_signal(barrier, inc=1, device_id=(q, me), device_id_type=MESH)

    def send_all(src_of, dst, ss, rs):
        for p in peers:
            pltpu.make_async_remote_copy(
                src_ref=src_of(p), dst_ref=dst, send_sem=ss, recv_sem=rs,
                device_id=(e_id, p), device_id_type=MESH,
            ).start()

    def wait_bytes(ref, sem):
        pltpu.make_async_copy(ref, ref, sem).wait()

    rt = rw[...] * rg[...]
    rt_s[...] = jnp.concatenate([rt[:8], rt[8:]], axis=1).astype(BF16)

    def merge(m):
        def group(g, _):
            es = pl.ds(g * GE, GE)
            wait_bytes(mbuf.at[m, es], load_sem.at[0, m * NG + g])
            wait_bytes(sbuf.at[m, es], load_sem.at[1, m * NG + g])

            def one(i, _):
                e = g * GE + i
                x = mbuf[m, e] + sbuf[m, e].astype(F32)
                mbuf[m, e] = x
                lmax[m, pl.ds(e, 1), :] = jnp.max(jnp.abs(x), axis=0, keepdims=True)
                return 0

            lax.fori_loop(0, GE, one, 0)
            return 0

        lax.fori_loop(0, NG, group, 0)
        for t in range(8):
            for q in range(4):
                rs_s[m, 4 * t + q] = jnp.concatenate(
                    [lmax[m, pl.ds(4 * k, 4), pl.ds(128 * t, 128)][:, 32 * q : 32 * q + 32] for k in range(4)], axis=1
                )

    def start_rs(m):
        send_all(lambda p: rs_s.at[m, p], rs_r.at[m, me], rs_ss.at[m], rs_rs.at[m])
        rs_r[m, me] = rs_s[m, me]

    scales = (cg, cu, cd)

    def finish_rs(m):
        wait_bytes(rs_r.at[m, pl.ds(0, N - 1)], rs_rs.at[m])
        top = jnp.max(rs_r[m], axis=0)
        ag_s[m] = top
        ag_r[m, me] = top
        for k in range(4):
            scales[m][pl.ds(4 * k, 4), :] = top[:, 32 * k : 32 * k + 32]
        send_all(lambda p: ag_s.at[m], ag_r.at[m, me], ag_ss.at[m], ag_rs.at[m])

    def finish_ag(m):
        wait_bytes(ag_r.at[m, pl.ds(0, N - 1)], ag_rs.at[m])
        for t in range(8):
            for k in range(4):
                row = jnp.concatenate([ag_r[m, 4 * t + q][:, 32 * k : 32 * k + 32] for q in range(4)], axis=1)
                row = 1.0 / row
                for i in range(4):
                    inv[m, 4 * k + i, :, pl.ds(128 * t, 128)] = row[i : i + 1]

    def send_group(m, g):
        gi = m * NG + g

        def pair(j, _):
            ea = g * GE + 2 * j + xhi
            eb = g * GE + 2 * j + 1 - xhi
            for t in range(8):
                cs = pl.ds(128 * t, 128)
                a = mbuf[m, ea, :, cs] * inv[m, ea, :, cs]
                b = mbuf[m, eb, :, cs] * inv[m, eb, :, cs]
                x = jnp.concatenate([a, b], axis=0).T.astype(BF16)
                snd[gi, pl.ds(4 * t, 4), j] = x.reshape(4, W, 128)
            return 0

        lax.fori_loop(0, GE // 2, pair, 0)
        send_all(lambda p: snd.at[gi, p], rcv.at[gi, me], d_ss.at[gi], d_rs.at[gi])
        rcv[gi, me] = snd[gi, me]

    outs = (og, ou, od)
    low = lax.broadcasted_iota(jnp.int32, (W, 128), 1) < 64

    def receive_group(m, g):
        gi = m * NG + g
        wait_bytes(rcv.at[gi, pl.ds(0, N - 1)], d_rs.at[gi])

        def tile(t, _):
            lanes = pl.ds(pl.multiple_of(t * 128, 128), 128)
            for j in range(GE // 2):
                a = rcv[gi, 2 * t, j].astype(F32)
                b = rcv[gi, 2 * t + 1, j].astype(F32)
                first = jnp.where(low, a, b)
                second = pltpu.roll(jnp.where(low, b, a), 64, 1)
                outs[m][g * GE + 2 * j, :, lanes] = first.astype(BF16)
                outs[m][g * GE + 2 * j + 1, :, lanes] = second.astype(BF16)
            return 0

        lax.fori_loop(0, N // 2, tile, 0)

    merge(0)
    pl.semaphore_wait(barrier, len(peers) + len(mates))
    start_rs(0)
    send_all(lambda p: rt_s, rt_r.at[me], rt_ss, rt_rs)
    rt_r[me] = rt_s[...]
    merge(1)
    start_rs(1)
    merge(2)
    start_rs(2)
    finish_rs(0)
    finish_rs(1)
    finish_rs(2)
    for m in range(3):
        finish_ag(m)

        def go(g, _):
            send_group(m, g)
            return 0

        lax.fori_loop(0, NG, go, 0)
        if m == 0:
            wait_bytes(rt_r.at[pl.ds(0, N - 1)], rt_rs)
            for t in range(16):
                a, b = rt_r[2 * t].astype(F32), rt_r[2 * t + 1].astype(F32)
                top = jnp.concatenate([a[:, :64], b[:, :64]], axis=1)
                bot = jnp.concatenate([a[:, 64:], b[:, 64:]], axis=1)
                rt_x[e_id, :, pl.ds(128 * t, 128)] = jnp.concatenate([top, bot], axis=0).astype(BF16)
            for i, q in enumerate(mates):
                pltpu.make_async_remote_copy(
                    src_ref=rt_x.at[e_id], dst_ref=rt_x.at[e_id], send_sem=rx_ss, recv_sem=rx_rs.at[i],
                    device_id=(q, me), device_id_type=MESH,
                ).start()
    for m in range(3):

        def come(g, _):
            receive_group(m, g)
            return 0

        lax.fori_loop(0, NG, come, 0)
        if m == 0:
            for i in range(3):
                wait_bytes(rt_x.at[0], rx_rs.at[i])
            for k in range(4):
                orr[pl.ds(16 * k, 16), :] = rt_x[k]
    wait_bytes(rt_x.at[pl.ds(0, 3)], rx_ss)
    wait_bytes(rt_r.at[pl.ds(0, N - 1)], rt_ss)
    for m in range(3):
        wait_bytes(rs_r.at[m, pl.ds(0, N - 1)], rs_ss.at[m])
        wait_bytes(ag_r.at[m, pl.ds(0, N - 1)], ag_ss.at[m])

    def drained(gi, _):
        wait_bytes(rcv.at[gi, pl.ds(0, N - 1)], d_ss.at[gi])
        return 0

    lax.fori_loop(0, 3 * NG, drained, 0)


def per_device(
    master_gate, second_gate, master_up, second_up, master_down, second_down, router_weight, router_gain
):
    vmem = pl.BlockSpec(memory_space=pltpu.VMEM)
    hbm = pl.BlockSpec(memory_space=pl.ANY)
    dma = pltpu.SemaphoreType.DMA
    big = jax.ShapeDtypeStruct((E, W, N * R), BF16)
    small = jax.ShapeDtypeStruct((E, W), F32)
    gate, up, down, cg, cu, cd, router = pl.pallas_call(
        kernel,
        out_shape=(big, big, big, small, small, small, jax.ShapeDtypeStruct((4 * E, N * R), BF16)),
        in_specs=[hbm] * 6 + [vmem] * 2,
        out_specs=(vmem,) * 7,
        scratch_shapes=[
            pltpu.VMEM((3, E, R, C), F32),
            pltpu.VMEM((3, E, R, C), BF16),
            pltpu.VMEM((3, E, C), F32),
            pltpu.VMEM((3, N, 4, 128), F32),
            pltpu.VMEM((3, N, 4, 128), F32),
            pltpu.VMEM((3, 4, 128), F32),
            pltpu.VMEM((3, N, 4, 128), F32),
            pltpu.VMEM((3, E, 1, C), F32),
            pltpu.VMEM((3 * NG, N, GE // 2, W, 128), BF16),
            pltpu.VMEM((3 * NG, N, GE // 2, W, 128), BF16),
            pltpu.VMEM((8, 128), BF16),
            pltpu.VMEM((N, 8, 128), BF16),
            pltpu.VMEM((4, 16, N * R), BF16),
            dma((2, 3 * NG)), dma((3,)), dma((3,)), dma((3,)), dma((3,)), dma((3 * NG,)), dma((3 * NG,)),
            dma, dma, dma, dma((3,)),
        ],
        compiler_params=pltpu.CompilerParams(
            collective_id=0, has_side_effects=True, vmem_limit_bytes=62 * 2**20
        ),
        name="reshard",
    )(
        master_gate, second_gate, master_up, second_up,
        jnp.swapaxes(master_down, 1, 2), jnp.swapaxes(second_down, 1, 2),
        router_weight.T, router_gain[None, :],
    )
    return (jnp.swapaxes(gate, 1, 2), jnp.swapaxes(up, 1, 2), down, cg, cu, cd, router.T)


def solution(mesh):
    wide, tall = P("expert", "shard", None), P("expert", None, "shard")
    return jax.shard_map(
        per_device,
        mesh=mesh,
        in_specs=(wide, wide, wide, wide, tall, tall, P("shard", "expert"), P("shard")),
        out_specs=(tall, tall, wide, P("expert", "shard"), P("expert", "shard"), P("expert", "shard"), P()),
        check_vma=False,
    )
```

time: 354 us -> 110 us (0.31)
  waiting for transfers between devices: 166 us -> 0 us
  Pallas kernels: 0 us -> 99.1 us
  local copies, waits for them, and re-layouts: 107 us -> 9.49 us
  starting transfers between devices: 32.4 us -> 0 us
  other arithmetic: 31.9 us -> 0 us
  between operations: 13.9 us -> 0.66 us
    all_gather x3 -> x0, waiting for transfers between devices: 160 us -> none  [over_pieces(): blocks = lax.all_gather(array, axis)]
    pallas_call x0 -> x1, Pallas kernels: none -> 99.1 us  [per_device(): pl.pallas_call(kernel, out_shape=(big, big, big, small, small, small, jax...]
    all_to_all x7 -> x0, local copies, waits for them, and re-layouts: 40.9 us -> none  [the longest x2 13.6 us: per_device(): lax.all_to_all(narrow_up, 'shard', split_axis=2, concat_axis=1, tiled=True)]
    unnamed x18 -> x19, local copies, waits for them, and re-layouts: 45.1 us -> 9.49 us
    all_to_all x5 -> x0, starting transfers between devices: 32.3 us -> none  [the longest x2 14.3 us: copy_for_each(): return lax.all_to_all(copies, axis, split_axis=0, concat_axis=0, tiled=True)]
    convert_element_type x3 -> x0, local copies, waits for them, and re-layouts: 18.5 us -> none  [the longest x1 6.17 us: per_device(): (merged_gate / jnp.expand_dims(scale_gate, 1)).astype(jnp.bfloat16)]
    reduce_max x6 -> x0, other arithmetic: 17.5 us -> none  [the longest x3 5.11 us: over_pieces(): return blocks.max(axis=0)]
    convert_element_type x4 -> x0, other arithmetic: 14.4 us -> none  [the longest x1 5 us: per_device(): (merged_up / jnp.expand_dims(scale_up, 1)).astype(jnp.bfloat16)]
  transfers between devices with their start and end apart: 8 -> 0, of which waited for: 4 -> 0; matrix products, arithmetic and copies ran while one was open for 28% -> 0% of each run, Pallas kernels for 0% -> 0%
where the time goes in v1:
time: 110 us; the launch traced here: 109 us
  Pallas kernels  99.1 us (90%)
  local copies, waits for them, and re-layouts  9.49 us (9%)
    pallas_call x1, Pallas kernels, per_device(): pl.pallas_call(kernel, out_shape=(big, big, big, small, small, small, jax...  99.1 us
    unnamed x19, local copies, waits for them, and re-layouts  9.49 us

profile of v1, /device:TPU:0, one launch (start us, length us, event | category | flops | bytes accessed | tf_op | source)
XLA Modules:
  0.0 109.2 jit_solution(5455777780922769880)
XLA Ops:
  0.6 99.1 %reshard.1 = (bf16[16,32,2048]{2,1,0:T(8,128)(2,1)}, bf16[16,32,2048]{2,1,0:T(8,128)(2,1)}, bf16[16,32,2048]{2,1,0:T(8,128)(2,1)}, f32[16,32]{1,0:T(8,128)}, f32...) custom-call(f32[16,64,1024]{2,1,0:T(8,128)} %mg.1, bf16[16,64,1024]{2,1,0:T(8,128)(2,1)} %sg.1, ...), custom_call_target="tpu_custom_call" | custom-call | tf_op jit(solution)/shard_map/reshard/pallas_call | solution.py:213
  99.7 0.0 copy-start.1
  99.7 3.3 %copy.22 = bf16[16,2048,32]{1,2,0:T(8,128)(2,1)} copy(bf16[16,2048,32]{1,2,0:T(8,128)(2,1)} %bitcast.10) | data formatting | bytes 4194304
  103.0 0.0 copy-done.1
  103.0 0.0 copy-start
  103.0 1.3 %copy.23 = bf16[16,2048,32]{1,2,0:T(8,128)(2,1)} copy(bf16[16,2048,32]{1,2,0:T(8,128)(2,1)S(1)} %bitcast.9) | data formatting | bytes 4194304
  104.3 1.0 copy-done
  105.4 0.0 copy-start.5
  105.4 0.0 copy-start.4
  105.4 0.0 copy-start.3
  105.4 0.0 copy-start.2
  105.4 1.3 %copy.24 = bf16[16,32,2048]{2,1,0:T(8,128)(2,1)} copy(bf16[16,32,2048]{2,1,0:T(8,128)(2,1)S(1)} %copy-done) | data formatting | bytes 4194304
  106.7 0.0 copy-done.5
  106.7 0.6 copy.25
  107.3 0.0 copy-done.4
  107.3 0.6 copy.26
  107.9 0.0 copy-done.3
  107.9 0.6 copy.27
  108.5 0.0 copy-done.2
  108.5 0.7 copy.28
Async XLA Ops:
  99.7 3.3 %copy-start.1 = (bf16[16,32,2048]{2,1,0:T(8,128)(2,1)S(1)}, bf16[16,32,2048]{2,1,0:T(8,128)(2,1)}, u32[]{:S(2)}) copy-start(bf16[16,32,2048]{2,1,0:T(8,128)(2,1)} %get-tuple-element.15) | copy-start | bytes 6291460
  103.0 2.3 %copy-start = (bf16[16,32,2048]{2,1,0:T(8,128)(2,1)S(1)}, bf16[16,32,2048]{2,1,0:T(8,128)(2,1)}, u32[]{:S(2)}) copy-start(bf16[16,32,2048]{2,1,0:T(8,128)(2,1)} %get-tuple-element.30) | copy-start | bytes 6291460
  105.4 1.3 %copy-start.5 = (f32[16,32]{1,0:T(8,128)S(1)}, f32[16,32]{1,0:T(8,128)}, u32[]{:S(2)}) copy-start(f32[16,32]{1,0:T(8,128)} %get-tuple-element.31) | copy-start | bytes 6148
  105.4 1.9 %copy-start.4 = (f32[16,32]{1,0:T(8,128)S(1)}, f32[16,32]{1,0:T(8,128)}, u32[]{:S(2)}) copy-start(f32[16,32]{1,0:T(8,128)} %get-tuple-element.32) | copy-start | bytes 6148
  105.4 2.5 %copy-start.3 = (f32[16,32]{1,0:T(8,128)S(1)}, f32[16,32]{1,0:T(8,128)}, u32[]{:S(2)}) copy-start(f32[16,32]{1,0:T(8,128)} %get-tuple-element.33) | copy-start | bytes 6148
  105.4 3.1 %copy-start.2 = (bf16[64,2048]{1,0:T(8,128)(2,1)S(1)}, bf16[64,2048]{1,0:T(8,128)(2,1)}, u32[]{:S(2)}) copy-start(bf16[64,2048]{1,0:T(8,128)(2,1)} %get-tuple-element.20) | copy-start | bytes 786436

commit v2 on v1

--- a/solution.py
+++ b/solution.py
@@ -12,6 +12,9 @@
 W = C // N
 GE = 4
 NG = E // GE
+TOP = 2.0 ** (127 / 16)
+TINY = 1e-30
+SMALL = 2.0**-126
 OFFSETS = [
     (dx, dy, dz) for dx in range(2) for dy in range(4) for dz in range(4) if (dx, dy, dz) != (0, 0, 0)
 ]
@@ -20,8 +23,8 @@
 def kernel(
     mg, sg, mu, su, md, sd, rw, rg,
     og, ou, od, cg, cu, cd, orr,
-    mbuf, sbuf, lmax, rs_s, rs_r, ag_s, ag_r, inv, snd, rcv, rt_s, rt_r, rt_x,
-    load_sem, rs_ss, rs_rs, ag_ss, ag_rs, d_ss, d_rs, rt_ss, rt_rs, rx_ss, rx_rs,
+    rwb, rgb, mbuf, sbuf, lmax, inl, fac, rs_s, rs_r, ag_s, ag_r, inv, snd, rcv, rt_s, rt_r, rt_x,
+    load_sem, rt_ld, rs_ss, rs_rs, ag_ss, ag_rs, d_ss, d_rs, rt_ss, rt_rs, rx_ss, rx_rs,
 ):
     e_id = lax.axis_index("expert")
     me = lax.axis_index("shard")
@@ -39,13 +42,20 @@
     peers = []
     for dx, dy, dz in OFFSETS:
         peers.append((lax.rem(z + dz, 4) * 4 + lax.rem(y + dy, 4)) * 2 + lax.rem(xhi + dx, 2))
-    mates = [lax.rem(e_id + k, 4) for k in range(1, 4)]
+    core = lax.rem(e_id, 2)
+    xlo = e_id // 2
+    other = (1 - xlo) * 2 + core
+    column = me - xhi
+    partner = (xlo * 2 + 1 - core, me)
+    right = (other, column + lax.rem(xhi + xlo, 2))
+    left = (other, column + lax.rem(xhi + 1 - xlo, 2))
+    mates = (partner, right, left)
 
     barrier = pltpu.get_barrier_semaphore()
     for p in peers:
         pl.semaphore_signal(barrier, inc=1, device_id=(e_id, p), device_id_type=MESH)
     for q in mates:
-        pl.semaphore_signal(barrier, inc=1, device_id=(q, me), device_id_type=MESH)
+        pl.semaphore_signal(barrier, inc=1, device_id=q, device_id_type=MESH)
 
     def send_all(src_of, dst, ss, rs):
         for p in peers:
@@ -54,11 +64,17 @@
                 device_id=(e_id, p), device_id_type=MESH,
             ).start()
 
+    def hop(ref, ss, rs, to):
+        return pltpu.make_async_remote_copy(
+            src_ref=ref, dst_ref=ref, send_sem=ss, recv_sem=rs, device_id=to, device_id_type=MESH
+        )
+
     def wait_bytes(ref, sem):
         pltpu.make_async_copy(ref, ref, sem).wait()
 
-    rt = rw[...] * rg[...]
-    rt_s[...] = jnp.concatenate([rt[:8], rt[8:]], axis=1).astype(BF16)
+    router_in = [pltpu.make_async_copy(a, b, rt_ld.at[i]) for i, (a, b) in enumerate(((rw, rwb), (rg, rgb)))]
+    for c in router_in:
+        c.start()
 
     def merge(m):
         def group(g, _):
@@ -107,7 +123,11 @@
                 for i in range(4):
                     inv[m, 4 * k + i, :, pl.ds(128 * t, 128)] = row[i : i + 1]
 
-    def send_group(m, g):
+    def launch(gi):
+        send_all(lambda p: snd.at[gi, p], rcv.at[gi, me], d_ss.at[gi], d_rs.at[gi])
+        rcv[gi, me] = snd[gi, me]
+
+    def stage(m, g, value):
         gi = m * NG + g
 
         def pair(j, _):
@@ -115,15 +135,56 @@
             eb = g * GE + 2 * j + 1 - xhi
             for t in range(8):
                 cs = pl.ds(128 * t, 128)
-                a = mbuf[m, ea, :, cs] * inv[m, ea, :, cs]
-                b = mbuf[m, eb, :, cs] * inv[m, eb, :, cs]
-                x = jnp.concatenate([a, b], axis=0).T.astype(BF16)
+                x = jnp.concatenate([value(ea, cs), value(eb, cs)], axis=0).T.astype(BF16)
                 snd[gi, pl.ds(4 * t, 4), j] = x.reshape(4, W, 128)
             return 0
 
         lax.fori_loop(0, GE // 2, pair, 0)
-        send_all(lambda p: snd.at[gi, p], rcv.at[gi, me], d_ss.at[gi], d_rs.at[gi])
-        rcv[gi, me] = snd[gi, me]
+
+    def send_group(m, g):
+        stage(m, g, lambda e, cs: mbuf[m, e, :, cs] * inv[m, e, :, cs])
+        launch(m * NG + g)
+
+    def encode(k, m, g):
+        for i in range(GE):
+            inl[k, i] = TOP / jnp.maximum(lmax[m, g * GE + i : g * GE + i + 1, :], TINY)
+
+        def value(e, cs):
+            v = mbuf[m, e, :, cs] * inl[k, e - g * GE, :, cs]
+            p = v * v
+            p = p * p
+            p = p * p
+            p = p * p
+            return jnp.where(v < 0, -p, p)
+
+        stage(m, g, value)
+
+    def decode(code, factor):
+        root = lax.rsqrt(lax.rsqrt(lax.rsqrt(lax.rsqrt(jnp.maximum(jnp.abs(code), SMALL))))) * factor
+        return jnp.where(code == 0, 0.0, jnp.where(code < 0, -root, root))
+
+    def receive_coded(k, m, g):
+        gi = m * NG + g
+        top = jnp.maximum(rs_r[m], TINY) / (ag_s[m][None] * TOP)
+        fac[k] = top.reshape(N * 4, 128).T[W * g : W * (g + 1)]
+        wait_bytes(rcv.at[gi, pl.ds(0, N - 1)], d_rs.at[gi])
+
+        def tile(t, _):
+            lanes = pl.ds(pl.multiple_of(t * 128, 128), 128)
+            here = pltpu.roll(fac[k], lax.rem(128 - 8 * t, 128), 1)
+            for j in range(GE // 2):
+                col = lambda i: jnp.broadcast_to(here[:, i : i + 1], (W, 128))
+                fa = jnp.where(low, col(2 * j), col(2 * j + 1))
+                fb = jnp.where(low, col(5 + 2 * j), col(4 + 2 * j))
+                a = decode(rcv[gi, 2 * t, j].astype(F32), fa)
+                b = decode(rcv[gi, 2 * t + 1, j].astype(F32), fb)
+                first = jnp.where(low, a, b)
+                second = pltpu.roll(jnp.where(low, b, a), 64, 1)
+                outs[m][g * GE + 2 * j, :, lanes] = first.astype(BF16)
+                outs[m][g * GE + 2 * j + 1, :, lanes] = second.astype(BF16)
+            return 0
+
+        lax.fori_loop(0, N // 2, tile, 0)
 
     outs = (og, ou, od)
     low = lax.broadcasted_iota(jnp.int32, (W, 128), 1) < 64
@@ -146,15 +207,23 @@
         lax.fori_loop(0, N // 2, tile, 0)
 
     merge(0)
+    encode(0, 0, 0)
     pl.semaphore_wait(barrier, len(peers) + len(mates))
     start_rs(0)
+    launch(0)
+    merge(1)
+    start_rs(1)
+    encode(1, 1, 0)
+    merge(2)
+    start_rs(2)
+    for c in router_in:
+        c.wait()
+    rt = rwb[...] * rgb[...]
+    rt_s[...] = jnp.concatenate([rt[:8], rt[8:]], axis=1).astype(BF16)
     send_all(lambda p: rt_s, rt_r.at[me], rt_ss, rt_rs)
     rt_r[me] = rt_s[...]
-    merge(1)
-    start_rs(1)
-    merge(2)
-    start_rs(2)
     finish_rs(0)
+    launch(NG)
     finish_rs(1)
     finish_rs(2)
     for m in range(3):
@@ -164,7 +233,7 @@
             send_group(m, g)
             return 0
 
-        lax.fori_loop(0, NG, go, 0)
+        lax.fori_loop(1 if m < 2 else 0, NG, go, 0)
         if m == 0:
             wait_bytes(rt_r.at[pl.ds(0, N - 1)], rt_rs)
             for t in range(16):
@@ -172,24 +241,33 @@
                 top = jnp.concatenate([a[:, :64], b[:, :64]], axis=1)
                 bot = jnp.concatenate([a[:, 64:], b[:, 64:]], axis=1)
                 rt_x[e_id, :, pl.ds(128 * t, 128)] = jnp.concatenate([top, bot], axis=0).astype(BF16)
-            for i, q in enumerate(mates):
-                pltpu.make_async_remote_copy(
-                    src_ref=rt_x.at[e_id], dst_ref=rt_x.at[e_id], send_sem=rx_ss, recv_sem=rx_rs.at[i],
-                    device_id=(q, me), device_id_type=MESH,
-                ).start()
-    for m in range(3):
-
-        def come(g, _):
+            hop(rt_x.at[e_id], rx_ss.at[0], rx_rs.at[0], partner).start()
+            hop(rt_x.at[e_id, :, pl.ds(0, 1024)], rx_ss.at[1], rx_rs.at[1], right).start()
+            hop(rt_x.at[e_id, :, pl.ds(1024, 1024)], rx_ss.at[2], rx_rs.at[2], left).start()
+    receive_coded(0, 0, 0)
+    receive_coded(1, 1, 0)
+
+    def come(m, start):
+        def one(g, _):
             receive_group(m, g)
             return 0
 
-        lax.fori_loop(0, NG, come, 0)
-        if m == 0:
-            for i in range(3):
-                wait_bytes(rt_x.at[0], rx_rs.at[i])
-            for k in range(4):
-                orr[pl.ds(16 * k, 16), :] = rt_x[k]
-    wait_bytes(rt_x.at[pl.ds(0, 3)], rx_ss)
+        lax.fori_loop(start, NG, one, 0)
+
+    come(0, 1)
+    wait_bytes(rt_x.at[0, :, pl.ds(0, 1024)], rx_rs.at[1])
+    wait_bytes(rt_x.at[0, :, pl.ds(0, 1024)], rx_rs.at[2])
+    hop(rt_x.at[other], rx_ss.at[3], rx_rs.at[3], partner).start()
+    come(1, 1)
+    wait_bytes(rt_x.at[0], rx_rs.at[0])
+    wait_bytes(rt_x.at[0], rx_rs.at[3])
+    for k in range(4):
+        orr[pl.ds(16 * k, 16), :] = rt_x[k]
+    come(2, 0)
+    wait_bytes(rt_x.at[0], rx_ss.at[0])
+    wait_bytes(rt_x.at[0, :, pl.ds(0, 1024)], rx_ss.at[1])
+    wait_bytes(rt_x.at[0, :, pl.ds(0, 1024)], rx_ss.at[2])
+    wait_bytes(rt_x.at[0], rx_ss.at[3])
     wait_bytes(rt_r.at[pl.ds(0, N - 1)], rt_ss)
     for m in range(3):
         wait_bytes(rs_r.at[m, pl.ds(0, N - 1)], rs_ss.at[m])
@@ -202,23 +280,37 @@
     lax.fori_loop(0, 3 * NG, drained, 0)
 
 
+def put_out(*refs):
+    sem = refs[14]
+    copies = [pltpu.make_async_copy(refs[i], refs[7 + i], sem.at[i]) for i in range(7)]
+    for c in copies:
+        c.start()
+    for c in copies:
+        c.wait()
+
+
 def per_device(
     master_gate, second_gate, master_up, second_up, master_down, second_down, router_weight, router_gain
 ):
     vmem = pl.BlockSpec(memory_space=pltpu.VMEM)
-    hbm = pl.BlockSpec(memory_space=pl.ANY)
+    hbm = pl.BlockSpec(memory_space=pltpu.HBM)
     dma = pltpu.SemaphoreType.DMA
     big = jax.ShapeDtypeStruct((E, W, N * R), BF16)
     small = jax.ShapeDtypeStruct((E, W), F32)
-    gate, up, down, cg, cu, cd, router = pl.pallas_call(
+    shapes = (big, big, big, small, small, small, jax.ShapeDtypeStruct((4 * E, N * R), BF16))
+    results = pl.pallas_call(
         kernel,
-        out_shape=(big, big, big, small, small, small, jax.ShapeDtypeStruct((4 * E, N * R), BF16)),
-        in_specs=[hbm] * 6 + [vmem] * 2,
+        out_shape=shapes,
+        in_specs=[hbm] * 8,
         out_specs=(vmem,) * 7,
         scratch_shapes=[
+            pltpu.VMEM((16, R), F32),
+            pltpu.VMEM((1, R), F32),
             pltpu.VMEM((3, E, R, C), F32),
             pltpu.VMEM((3, E, R, C), BF16),
             pltpu.VMEM((3, E, C), F32),
+            pltpu.VMEM((2, GE, 1, C), F32),
+            pltpu.VMEM((2, W, 128), F32),
             pltpu.VMEM((3, N, 4, 128), F32),
             pltpu.VMEM((3, N, 4, 128), F32),
             pltpu.VMEM((3, 4, 128), F32),
@@ -229,11 +321,11 @@
             pltpu.VMEM((8, 128), BF16),
             pltpu.VMEM((N, 8, 128), BF16),
             pltpu.VMEM((4, 16, N * R), BF16),
-            dma((2, 3 * NG)), dma((3,)), dma((3,)), dma((3,)), dma((3,)), dma((3 * NG,)), dma((3 * NG,)),
-            dma, dma, dma, dma((3,)),
+            dma((2, 3 * NG)), dma((2,)), dma((3,)), dma((3,)), dma((3,)), dma((3,)), dma((3 * NG,)), dma((3 * NG,)),
+            dma, dma, dma((4,)), dma((4,)),
         ],
         compiler_params=pltpu.CompilerParams(
-            collective_id=0, has_side_effects=True, vmem_limit_bytes=62 * 2**20
+            collective_id=0, has_side_effects=True, vmem_limit_bytes=47308 * 2**10
         ),
         name="reshard",
     )(
@@ -241,6 +333,15 @@
         jnp.swapaxes(master_down, 1, 2), jnp.swapaxes(second_down, 1, 2),
         router_weight.T, router_gain[None, :],
     )
+    gate, up, down, cg, cu, cd, router = pl.pallas_call(
+        put_out,
+        out_shape=shapes,
+        in_specs=[vmem] * 7,
+        out_specs=(hbm,) * 7,
+        scratch_shapes=[dma((7,))],
+        compiler_params=pltpu.CompilerParams(vmem_limit_bytes=4 * 2**20),
+        name="put_out",
+    )(*results)
     return (jnp.swapaxes(gate, 1, 2), jnp.swapaxes(up, 1, 2), down, cg, cu, cd, router.T)
 
 

time: 110 us -> 92.7 us (0.84)
  Pallas kernels: 99.1 us -> 90.5 us
  local copies, waits for them, and re-layouts: 9.49 us -> 1.34 us
    pallas_call x1 -> x2, Pallas kernels: 99.1 us -> 90.5 us  [the longest x1 87.7 us: per_device(): pl.pallas_call(kernel, out_shape=shapes, in_specs=[hbm] * 8, out_specs=(v...]
    unnamed x19 -> x4, local copies, waits for them, and re-layouts: 9.49 us -> 1.34 us
where the time goes in v2:
time: 92.7 us; the launch traced here: 92.5 us
  Pallas kernels  90.5 us (98%)
  local copies, waits for them, and re-layouts  1.34 us (1%)
    pallas_call x1, Pallas kernels, per_device(): pl.pallas_call(kernel, out_shape=shapes, in_specs=[hbm] * 8, out_specs=(v...  87.7 us
    pallas_call x1, Pallas kernels, per_device(): pl.pallas_call(put_out, out_shape=shapes, in_specs=[vmem] * 7, out_specs=...  2.79 us

profile of v2, /device:TPU:0, one launch (start us, length us, event | category | flops | bytes accessed | tf_op | source)
XLA Modules:
  0.0 92.5 jit_solution(17213828432209700863)
XLA Ops:
  0.6 0.0 copy-start
  0.6 0.7 copy-done
  1.3 0.0 copy-start.1
  1.3 0.7 copy-done.1
  2.0 87.7 %reshard.1 = (bf16[16,32,2048]{2,1,0:T(8,128)(2,1)S(1)}, bf16[16,32,2048]{2,1,0:T(8,128)(2,1)S(1)}, bf16[16,32,2048]{2,1,0:T(8,128)(2,1)S(1)}, f32[16,32]{1,0:T(...) custom-call(f32[16,64,1024]{2,1,0:T(8,128)} %mg.1, ...), custom_call_target="tpu_custom_call" | custom-call | tf_op jit(solution)/shard_map/reshard/pallas_call | solution.py:301
  89.7 2.8 %put_out.1 = (bf16[16,32,2048]{2,1,0:T(8,128)(2,1)}, bf16[16,32,2048]{2,1,0:T(8,128)(2,1)}, bf16[16,32,2048]{2,1,0:T(8,128)(2,1)}, f32[16,32]{1,0:T(8,128)}, f32...) custom-call(bf16[16,32,2048]{2,1,0:T(8,128)(2,1)S(1)} %get-tuple-element.21.refs_0_, ...), custom_call_target="tpu_custom_call" | custom-call | tf_op jit(solution)/shard_map/put_out/pallas_call | solution.py:336
Async XLA Ops:
  0.6 0.7 copy-start
  1.3 0.7 copy-start.1

commit v3 on v2

--- a/solution.py
+++ b/solution.py
@@ -20,10 +20,17 @@
 ]
 
 
+def joined(a, b):
+    low = lax.broadcasted_iota(jnp.int32, (W, 128), 1) < 64
+    first = jnp.where(low, a, b)
+    second = pltpu.roll(jnp.where(low, b, a), 64, 1)
+    return first.astype(BF16), second.astype(BF16)
+
+
 def kernel(
     mg, sg, mu, su, md, sd, rw, rg,
-    og, ou, od, cg, cu, cd, orr,
-    rwb, rgb, mbuf, sbuf, lmax, inl, fac, rs_s, rs_r, ag_s, ag_r, inv, snd, rcv, rt_s, rt_r, rt_x,
+    og, ou, od, cg, cu, cd, orr, last,
+    rwb, rgb, mbuf, sbuf, lmax, inl, fac, rs_s, rs_r, whole, ag_s, ag_r, inv, snd, rcv, rt_s, rt_r, rt_x,
     load_sem, rt_ld, rs_ss, rs_rs, ag_ss, ag_rs, d_ss, d_rs, rt_ss, rt_rs, rx_ss, rx_rs,
 ):
     e_id = lax.axis_index("expert")
@@ -76,30 +83,30 @@
     for c in router_in:
         c.start()
 
-    def merge(m):
+    def merge(m, start, stop):
         def group(g, _):
             es = pl.ds(g * GE, GE)
             wait_bytes(mbuf.at[m, es], load_sem.at[0, m * NG + g])
             wait_bytes(sbuf.at[m, es], load_sem.at[1, m * NG + g])
 
-            def one(i, _):
-                e = g * GE + i
+            def one(k, _):
+                e = g * GE + k
                 x = mbuf[m, e] + sbuf[m, e].astype(F32)
                 mbuf[m, e] = x
-                lmax[m, pl.ds(e, 1), :] = jnp.max(jnp.abs(x), axis=0, keepdims=True)
+                lmax[m, k, pl.ds(g, 1), :] = jnp.max(jnp.abs(x), axis=0, keepdims=True)
                 return 0
 
             lax.fori_loop(0, GE, one, 0)
             return 0
 
-        lax.fori_loop(0, NG, group, 0)
+        lax.fori_loop(start, stop, group, 0)
+
+    def start_rs(m):
         for t in range(8):
             for q in range(4):
                 rs_s[m, 4 * t + q] = jnp.concatenate(
-                    [lmax[m, pl.ds(4 * k, 4), pl.ds(128 * t, 128)][:, 32 * q : 32 * q + 32] for k in range(4)], axis=1
+                    [lmax[m, k, :, pl.ds(128 * t, 128)][:, 32 * q : 32 * q + 32] for k in range(GE)], axis=1
                 )
-
-    def start_rs(m):
         send_all(lambda p: rs_s.at[m, p], rs_r.at[m, me], rs_ss.at[m], rs_rs.at[m])
         rs_r[m, me] = rs_s[m, me]
 
@@ -108,20 +115,25 @@
     def finish_rs(m):
         wait_bytes(rs_r.at[m, pl.ds(0, N - 1)], rs_rs.at[m])
         top = jnp.max(rs_r[m], axis=0)
-        ag_s[m] = top
-        ag_r[m, me] = top
-        for k in range(4):
-            scales[m][pl.ds(4 * k, 4), :] = top[:, 32 * k : 32 * k + 32]
+        whole[m] = top
+        ag_s[m] = top[1:]
+        ag_r[m, me] = top[1:]
         send_all(lambda p: ag_s.at[m], ag_r.at[m, me], ag_ss.at[m], ag_rs.at[m])
+
+    def put_scale(m):
+        top = whole[m]
+        for i in range(NG):
+            for k in range(GE):
+                scales[m][4 * i + k : 4 * i + k + 1, :] = top[i : i + 1, 32 * k : 32 * k + 32]
 
     def finish_ag(m):
         wait_bytes(ag_r.at[m, pl.ds(0, N - 1)], ag_rs.at[m])
         for t in range(8):
-            for k in range(4):
+            for k in range(GE):
                 row = jnp.concatenate([ag_r[m, 4 * t + q][:, 32 * k : 32 * k + 32] for q in range(4)], axis=1)
                 row = 1.0 / row
-                for i in range(4):
-                    inv[m, 4 * k + i, :, pl.ds(128 * t, 128)] = row[i : i + 1]
+                for i in range(1, NG):
+                    inv[m, 4 * i + k, :, pl.ds(128 * t, 128)] = row[i - 1 : i]
 
     def launch(gi):
         send_all(lambda p: snd.at[gi, p], rcv.at[gi, me], d_ss.at[gi], d_rs.at[gi])
@@ -145,43 +157,45 @@
         stage(m, g, lambda e, cs: mbuf[m, e, :, cs] * inv[m, e, :, cs])
         launch(m * NG + g)
 
-    def encode(k, m, g):
-        for i in range(GE):
-            inl[k, i] = TOP / jnp.maximum(lmax[m, g * GE + i : g * GE + i + 1, :], TINY)
+    def encode(m):
+        for k in range(GE):
+            inl[m, k] = TOP / jnp.maximum(lmax[m, k, 0:1, :], TINY)
 
         def value(e, cs):
-            v = mbuf[m, e, :, cs] * inl[k, e - g * GE, :, cs]
+            v = mbuf[m, e, :, cs] * inl[m, e, :, cs]
             p = v * v
             p = p * p
             p = p * p
             p = p * p
             return jnp.where(v < 0, -p, p)
 
-        stage(m, g, value)
+        stage(m, 0, value)
 
     def decode(code, factor):
         root = lax.rsqrt(lax.rsqrt(lax.rsqrt(lax.rsqrt(jnp.maximum(jnp.abs(code), SMALL))))) * factor
         return jnp.where(code == 0, 0.0, jnp.where(code < 0, -root, root))
 
-    def receive_coded(k, m, g):
-        gi = m * NG + g
-        top = jnp.maximum(rs_r[m], TINY) / (ag_s[m][None] * TOP)
-        fac[k] = top.reshape(N * 4, 128).T[W * g : W * (g + 1)]
+    def receive_coded(m):
+        gi = m * NG
+        top = jnp.maximum(rs_r[m][:, 0, :], TINY) / (whole[m][0:1, :] * TOP)
+        top = jnp.concatenate([top, jnp.zeros((128 - N, 128), F32)], axis=0).T
+        for k in range(GE):
+            fac[k] = top[W * k : W * k + W]
         wait_bytes(rcv.at[gi, pl.ds(0, N - 1)], d_rs.at[gi])
 
         def tile(t, _):
             lanes = pl.ds(pl.multiple_of(t * 128, 128), 128)
-            here = pltpu.roll(fac[k], lax.rem(128 - 8 * t, 128), 1)
+            here = [pltpu.roll(fac[k], lax.rem(128 - 2 * t, 128), 1) for k in range(GE)]
+            even = [jnp.broadcast_to(h[:, 0:1], (W, 128)) for h in here]
+            odd = [jnp.broadcast_to(h[:, 1:2], (W, 128)) for h in here]
             for j in range(GE // 2):
-                col = lambda i: jnp.broadcast_to(here[:, i : i + 1], (W, 128))
-                fa = jnp.where(low, col(2 * j), col(2 * j + 1))
-                fb = jnp.where(low, col(5 + 2 * j), col(4 + 2 * j))
+                fa = jnp.where(low, even[2 * j], even[2 * j + 1])
+                fb = jnp.where(low, odd[2 * j + 1], odd[2 * j])
                 a = decode(rcv[gi, 2 * t, j].astype(F32), fa)
                 b = decode(rcv[gi, 2 * t + 1, j].astype(F32), fb)
-                first = jnp.where(low, a, b)
-                second = pltpu.roll(jnp.where(low, b, a), 64, 1)
-                outs[m][g * GE + 2 * j, :, lanes] = first.astype(BF16)
-                outs[m][g * GE + 2 * j + 1, :, lanes] = second.astype(BF16)
+                first, second = joined(a, b)
+                outs[m][2 * j, :, lanes] = first
+                outs[m][2 * j + 1, :, lanes] = second
             return 0
 
         lax.fori_loop(0, N // 2, tile, 0)
@@ -196,34 +210,36 @@
         def tile(t, _):
             lanes = pl.ds(pl.multiple_of(t * 128, 128), 128)
             for j in range(GE // 2):
-                a = rcv[gi, 2 * t, j].astype(F32)
-                b = rcv[gi, 2 * t + 1, j].astype(F32)
-                first = jnp.where(low, a, b)
-                second = pltpu.roll(jnp.where(low, b, a), 64, 1)
-                outs[m][g * GE + 2 * j, :, lanes] = first.astype(BF16)
-                outs[m][g * GE + 2 * j + 1, :, lanes] = second.astype(BF16)
+                first, second = joined(rcv[gi, 2 * t, j].astype(F32), rcv[gi, 2 * t + 1, j].astype(F32))
+                outs[m][g * GE + 2 * j, :, lanes] = first
+                outs[m][g * GE + 2 * j + 1, :, lanes] = second
             return 0
 
         lax.fori_loop(0, N // 2, tile, 0)
 
-    merge(0)
-    encode(0, 0, 0)
+    merge(0, 0, 1)
+    encode(0)
     pl.semaphore_wait(barrier, len(peers) + len(mates))
+    launch(0)
+    merge(0, 1, NG)
     start_rs(0)
-    launch(0)
-    merge(1)
+    merge(1, 0, 1)
+    encode(1)
+    launch(NG)
+    merge(1, 1, NG)
     start_rs(1)
-    encode(1, 1, 0)
-    merge(2)
+    merge(2, 0, 1)
+    encode(2)
+    merge(2, 1, NG)
     start_rs(2)
+    finish_rs(0)
+    launch(2 * NG)
     for c in router_in:
         c.wait()
     rt = rwb[...] * rgb[...]
     rt_s[...] = jnp.concatenate([rt[:8], rt[8:]], axis=1).astype(BF16)
     send_all(lambda p: rt_s, rt_r.at[me], rt_ss, rt_rs)
     rt_r[me] = rt_s[...]
-    finish_rs(0)
-    launch(NG)
     finish_rs(1)
     finish_rs(2)
     for m in range(3):
@@ -233,7 +249,7 @@
             send_group(m, g)
             return 0
 
-        lax.fori_loop(1 if m < 2 else 0, NG, go, 0)
+        lax.fori_loop(1, NG, go, 0)
         if m == 0:
             wait_bytes(rt_r.at[pl.ds(0, N - 1)], rt_rs)
             for t in range(16):
@@ -244,26 +260,29 @@
             hop(rt_x.at[e_id], rx_ss.at[0], rx_rs.at[0], partner).start()
             hop(rt_x.at[e_id, :, pl.ds(0, 1024)], rx_ss.at[1], rx_rs.at[1], right).start()
             hop(rt_x.at[e_id, :, pl.ds(1024, 1024)], rx_ss.at[2], rx_rs.at[2], left).start()
-    receive_coded(0, 0, 0)
-    receive_coded(1, 1, 0)
-
-    def come(m, start):
+    for m in range(3):
+        receive_coded(m)
+        put_scale(m)
+
+    def come(m, stop):
         def one(g, _):
             receive_group(m, g)
             return 0
 
-        lax.fori_loop(start, NG, one, 0)
-
-    come(0, 1)
+        lax.fori_loop(1, stop, one, 0)
+
+    come(0, NG)
     wait_bytes(rt_x.at[0, :, pl.ds(0, 1024)], rx_rs.at[1])
     wait_bytes(rt_x.at[0, :, pl.ds(0, 1024)], rx_rs.at[2])
     hop(rt_x.at[other], rx_ss.at[3], rx_rs.at[3], partner).start()
-    come(1, 1)
+    come(1, NG)
     wait_bytes(rt_x.at[0], rx_rs.at[0])
     wait_bytes(rt_x.at[0], rx_rs.at[3])
     for k in range(4):
         orr[pl.ds(16 * k, 16), :] = rt_x[k]
-    come(2, 0)
+    come(2, NG - 1)
+    wait_bytes(rcv.at[3 * NG - 1, pl.ds(0, N - 1)], d_rs.at[3 * NG - 1])
+    last[...] = rcv[3 * NG - 1]
     wait_bytes(rt_x.at[0], rx_ss.at[0])
     wait_bytes(rt_x.at[0, :, pl.ds(0, 1024)], rx_ss.at[1])
     wait_bytes(rt_x.at[0, :, pl.ds(0, 1024)], rx_ss.at[2])
@@ -280,11 +299,21 @@
     lax.fori_loop(0, 3 * NG, drained, 0)
 
 
-def put_out(*refs):
-    sem = refs[14]
-    copies = [pltpu.make_async_copy(refs[i], refs[7 + i], sem.at[i]) for i in range(7)]
+def put_out(og, ou, od, cg, cu, cd, orr, last, hg, hu, hd, hcg, hcu, hcd, hr, tail, sem):
+    done = pl.ds(0, E - GE)
+    rest = pl.ds(E - GE, GE)
+    pairs = ((og, hg), (ou, hu), (od.at[done], hd.at[done]), (cg, hcg), (cu, hcu), (cd, hcd), (orr, hr))
+    copies = [pltpu.make_async_copy(a, b, sem.at[i]) for i, (a, b) in enumerate(pairs)]
     for c in copies:
         c.start()
+    for t in range(N // 2):
+        lanes = pl.ds(128 * t, 128)
+        for j in range(GE // 2):
+            first, second = joined(last[2 * t, j].astype(F32), last[2 * t + 1, j].astype(F32))
+            tail[2 * j, :, lanes] = first
+            tail[2 * j + 1, :, lanes] = second
+    copies.append(pltpu.make_async_copy(tail, hd.at[rest], sem.at[7]))
+    copies[-1].start()
     for c in copies:
         c.wait()
 
@@ -297,24 +326,26 @@
     dma = pltpu.SemaphoreType.DMA
     big = jax.ShapeDtypeStruct((E, W, N * R), BF16)
     small = jax.ShapeDtypeStruct((E, W), F32)
+    raw = jax.ShapeDtypeStruct((N, GE // 2, W, 128), BF16)
     shapes = (big, big, big, small, small, small, jax.ShapeDtypeStruct((4 * E, N * R), BF16))
     results = pl.pallas_call(
         kernel,
-        out_shape=shapes,
+        out_shape=shapes + (raw,),
         in_specs=[hbm] * 8,
-        out_specs=(vmem,) * 7,
+        out_specs=(vmem,) * 8,
         scratch_shapes=[
             pltpu.VMEM((16, R), F32),
             pltpu.VMEM((1, R), F32),
             pltpu.VMEM((3, E, R, C), F32),
             pltpu.VMEM((3, E, R, C), BF16),
-            pltpu.VMEM((3, E, C), F32),
-            pltpu.VMEM((2, GE, 1, C), F32),
-            pltpu.VMEM((2, W, 128), F32),
-            pltpu.VMEM((3, N, 4, 128), F32),
-            pltpu.VMEM((3, N, 4, 128), F32),
-            pltpu.VMEM((3, 4, 128), F32),
-            pltpu.VMEM((3, N, 4, 128), F32),
+            pltpu.VMEM((3, GE, NG, C), F32),
+            pltpu.VMEM((3, GE, 1, C), F32),
+            pltpu.VMEM((GE, W, 128), F32),
+            pltpu.VMEM((3, N, NG, 128), F32),
+            pltpu.VMEM((3, N, NG, 128), F32),
+            pltpu.VMEM((3, NG, 128), F32),
+            pltpu.VMEM((3, NG - 1, 128), F32),
+            pltpu.VMEM((3, N, NG - 1, 128), F32),
             pltpu.VMEM((3, E, 1, C), F32),
             pltpu.VMEM((3 * NG, N, GE // 2, W, 128), BF16),
             pltpu.VMEM((3 * NG, N, GE // 2, W, 128), BF16),
@@ -325,20 +356,25 @@
             dma, dma, dma((4,)), dma((4,)),
         ],
         compiler_params=pltpu.CompilerParams(
-            collective_id=0, has_side_effects=True, vmem_limit_bytes=47308 * 2**10
+            collective_id=0, has_side_effects=True, vmem_limit_bytes=44 * 2**20
         ),
         name="reshard",
     )(
-        master_gate, second_gate, master_up, second_up,
-        jnp.swapaxes(master_down, 1, 2), jnp.swapaxes(second_down, 1, 2),
-        router_weight.T, router_gain[None, :],
+        *(
+            pltpu.with_memory_space_constraint(x, pltpu.HBM)
+            for x in (
+                master_gate, second_gate, master_up, second_up,
+                jnp.swapaxes(master_down, 1, 2), jnp.swapaxes(second_down, 1, 2),
+                router_weight.T, router_gain[None, :],
+            )
+        )
     )
     gate, up, down, cg, cu, cd, router = pl.pallas_call(
         put_out,
         out_shape=shapes,
-        in_specs=[vmem] * 7,
+        in_specs=[vmem] * 8,
         out_specs=(hbm,) * 7,
-        scratch_shapes=[dma((7,))],
+        scratch_shapes=[pltpu.VMEM((GE, W, N * R), BF16), dma((8,))],
         compiler_params=pltpu.CompilerParams(vmem_limit_bytes=4 * 2**20),
         name="put_out",
     )(*results)

time: 92.7 us -> 88.8 us (0.958)
  Pallas kernels: 90.5 us -> 88 us
  local copies, waits for them, and re-layouts: 1.34 us -> 0 us
    pallas_call x2, Pallas kernels: 90.5 us -> 88 us  [the longest x1 85.2 us: per_device(): pl.pallas_call(kernel, out_shape=shapes + (raw,), in_specs=[hbm] * 8, out...]
    unnamed x4 -> x0, local copies, waits for them, and re-layouts: 1.34 us -> none
where the time goes in v3:
time: 88.8 us; the launch traced here: 88.7 us
  Pallas kernels  88 us (99%)
    pallas_call x1, Pallas kernels, per_device(): pl.pallas_call(kernel, out_shape=shapes + (raw,), in_specs=[hbm] * 8, out...  85.2 us
    pallas_call x1, Pallas kernels, per_device(): pl.pallas_call(put_out, out_shape=shapes, in_specs=[vmem] * 8, out_specs=...  2.81 us

profile of v3, /device:TPU:0, one launch (start us, length us, event | category | flops | bytes accessed | tf_op | source)
XLA Modules:
  0.0 88.7 jit_solution(7850132183658233625)
XLA Ops:
  0.6 85.2 %reshard.1 = (bf16[16,32,2048]{2,1,0:T(8,128)(2,1)S(1)}, bf16[16,32,2048]{2,1,0:T(8,128)(2,1)S(1)}, bf16[16,32,2048]{2,1,0:T(8,128)(2,1)S(1)}, f32[16,32]{1,0:T(...) custom-call(f32[16,64,1024]{2,1,0:T(8,128)} %mg.1, ...), custom_call_target="tpu_custom_call" | custom-call | tf_op jit(solution)/shard_map/reshard/pallas_call | solution.py:331
  85.8 2.8 %put_out.1 = (bf16[16,32,2048]{2,1,0:T(8,128)(2,1)}, bf16[16,32,2048]{2,1,0:T(8,128)(2,1)}, bf16[16,32,2048]{2,1,0:T(8,128)(2,1)}, f32[16,32]{1,0:T(8,128)}, f32...) custom-call(bf16[16,32,2048]{2,1,0:T(8,128)(2,1)S(1)} %get-tuple-element.22.og, ...), custom_call_target="tpu_custom_call" | custom-call | tf_op jit(solution)/shard_map/put_out/pallas_call | solution.py:372

commit v4 on v3

v4 whole, which is shorter than its diff:
```python
import jax
import jax.numpy as jnp
from jax import lax
from jax.experimental import pallas as pl
from jax.experimental.pallas import tpu as pltpu
from jax.sharding import PartitionSpec as P

MESH = pl.DeviceIdType.MESH
F32, BF16 = jnp.float32, jnp.bfloat16
N = 32
E, R, C = 16, 64, 1024
W = C // N
GE = 4
NG = E // GE
TOP = 2.0 ** (79 / 16)
SPLIT = 2.0**31
TINY = 1e-30


def hops(offset):
    dx, dy, dz = offset
    return 2 * dx + min(dy, 4 - dy) + min(dz, 4 - dz)


OFFSETS = sorted(
    [(dx, dy, dz) for dx in range(2) for dy in range(4) for dz in range(4) if (dx, dy, dz) != (0, 0, 0)],
    key=hops,
    reverse=True,
)
AHEAD = 4
FAR = sum(hops(o) > 3 for o in OFFSETS)


def decode(code, factor):
    level = jnp.log2(jnp.abs(code))
    size = jnp.exp2(jnp.minimum(level * (1 / 32) - 127 / 32, level * (1 / 16) - 79 / 16)) * factor
    return jnp.where(code < 0, -size, size)


def decoded(t, codes, fac):
    low = lax.broadcasted_iota(jnp.int32, (W, 128), 1) < 64
    even = [jnp.broadcast_to(fac[k][:, 2 * t : 2 * t + 1], (W, 128)) for k in range(GE)]
    odd = [jnp.broadcast_to(fac[k][:, 2 * t + 1 : 2 * t + 2], (W, 128)) for k in range(GE)]
    found = []
    for j in range(GE // 2):
        fa = jnp.where(low, even[2 * j], even[2 * j + 1])
        fb = jnp.where(low, odd[2 * j + 1], odd[2 * j])
        a = decode(codes[2 * t, j].astype(F32), fa)
        b = decode(codes[2 * t + 1, j].astype(F32), fb)
        found.append(jnp.where(low, a, b).astype(BF16))
        found.append(pltpu.roll(jnp.where(low, b, a), 64, 1).astype(BF16))
    return found


def kernel(
    mg, sg, mu, su, md, sd, rw, rg,
    og, ou, od, cg, cu, cd, orr, last, lfac,
    rwb, rgb, mbuf, sbuf, lmax, inl, fac, rs_s, rs_r, snd, rcv, rt_s, rt_r, rt_x,
    load_sem, rt_ld, rs_ss, rs_rs, ready, d_ss, d_rs, rt_ss, rt_rs, rx_ss, rx_rs,
):
    e_id = lax.axis_index("expert")
    me = lax.axis_index("shard")
    xhi = lax.rem(me, 2)
    y = lax.rem(me // 2, 4)
    z = me // 8

    masters, seconds = (mg, mu, md), (sg, su, sd)
    for m in range(3):
        for g in range(NG):
            es = pl.ds(g * GE, GE)
            pltpu.make_async_copy(masters[m].at[es], mbuf.at[m, es], load_sem.at[0, m * NG + g]).start()
            pltpu.make_async_copy(seconds[m].at[es], sbuf.at[m, es], load_sem.at[1, m * NG + g]).start()

    peers = []
    for dx, dy, dz in OFFSETS:
        peers.append((lax.rem(z + dz, 4) * 4 + lax.rem(y + dy, 4)) * 2 + lax.rem(xhi + dx, 2))
    core = lax.rem(e_id, 2)
    xlo = e_id // 2
    other = (1 - xlo) * 2 + core
    column = me - xhi
    partner = (xlo * 2 + 1 - core, me)
    right = (other, column + lax.rem(xhi + xlo, 2))
    left = (other, column + lax.rem(xhi + 1 - xlo, 2))
    mates = (partner, right, left)

    barrier = pltpu.get_barrier_semaphore()
    for p in peers:
        pl.semaphore_signal(barrier, inc=1, device_id=(e_id, p), device_id_type=MESH)
    for q in mates:
        pl.semaphore_signal(barrier, inc=1, device_id=q, device_id_type=MESH)

    def send_all(src_of, dst, ss, rs, to=peers):
        for p in to:
            pltpu.make_async_remote_copy(
                src_ref=src_of(p), dst_ref=dst, send_sem=ss, recv_sem=rs,
                device_id=(e_id, p), device_id_type=MESH,
            ).start()

    def hop(ref, ss, rs, to):
        return pltpu.make_async_remote_copy(
            src_ref=ref, dst_ref=ref, send_sem=ss, recv_sem=rs, device_id=to, device_id_type=MESH
        )

    def wait_bytes(ref, sem):
        pltpu.make_async_copy(ref, ref, sem).wait()

    router_in = [pltpu.make_async_copy(a, b, rt_ld.at[i]) for i, (a, b) in enumerate(((rw, rwb), (rg, rgb)))]
    for c in router_in:
        c.start()

    def merge(m, start):
        def group(g, _):
            gi = m * NG + g
            es = pl.ds(g * GE, GE)
            wait_bytes(mbuf.at[m, es], load_sem.at[0, gi])
            wait_bytes(sbuf.at[m, es], load_sem.at[1, gi])

            def one(k, _):
                e = g * GE + k
                x = mbuf[m, e] + sbuf[m, e].astype(F32)
                mbuf[m, e] = x
                row = jnp.max(jnp.abs(x), axis=0, keepdims=True)
                lmax[m, k, pl.ds(g, 1), :] = row
                inl[m, e] = TOP / jnp.maximum(row, TINY)
                return 0

            lax.fori_loop(0, GE, one, 0)
            return 0

        lax.fori_loop(start, NG if start or m else 1, group, 0)

    def stage(m, g):
        gi = m * NG + g

        def coded(k, cs):
            e = g * GE + k
            v = mbuf[m, e, :, cs] * inl[m, e, :, cs]
            p = v * v
            p = p * p
            p = p * p
            p = p * p
            p = jnp.where(p < SPLIT, p, p * (p * (1 / SPLIT)))
            return jnp.where(v < 0, -p, p)

        def pair(j, _):
            for t in range(8):
                cs = pl.ds(128 * t, 128)
                x = jnp.concatenate([coded(2 * j + xhi, cs), coded(2 * j + 1 - xhi, cs)], axis=0).T.astype(BF16)
                snd[gi, pl.ds(4 * t, 4), j] = x.reshape(4, W, 128)
            return 0

        lax.fori_loop(0, GE // 2, pair, 0)
        rcv[gi, me] = snd[gi, me]

    def launch(gi, to):
        send_all(lambda p: snd.at[gi, p], rcv.at[gi, me], d_ss.at[gi], d_rs.at[gi], to)

    def start_rs(m):
        for t in range(8):
            for q in range(4):
                rs_s[m, 4 * t + q] = jnp.concatenate(
                    [lmax[m, k, :, pl.ds(128 * t, 128)][:, 32 * q : 32 * q + 32] for k in range(GE)], axis=1
                )
        send_all(lambda p: rs_s.at[m, p], rs_r.at[m, me], rs_ss.at[m], rs_rs.at[m])
        rs_r[m, me] = rs_s[m, me]

    scales = (cg, cu, cd)

    def finish_rs(m):
        wait_bytes(rs_r.at[m, pl.ds(0, N - 1)], rs_rs.at[m])
        top = jnp.max(rs_r[m], axis=0)
        for i in range(NG):
            for k in range(GE):
                scales[m][4 * i + k : 4 * i + k + 1, :] = top[i : i + 1, 32 * k : 32 * k + 32]
            f = jnp.maximum(rs_r[m][:, i, :], TINY) / top[i : i + 1]
            f = jnp.concatenate([f, jnp.zeros((128 - N, 128), F32)], axis=0).T
            for k in range(GE):
                fac[i, k] = f[W * k : W * k + W]

    outs = (og, ou, od)
    def receive(m, g):
        gi = m * NG + g
        wait_bytes(rcv.at[gi, pl.ds(0, N - 1)], d_rs.at[gi])

        for t in range(N // 2):
            for i, x in enumerate(decoded(t, rcv.at[gi], fac.at[g])):
                outs[m][g * GE + i, :, pl.ds(128 * t, 128)] = x

    def drain(gi):
        wait_bytes(rcv.at[gi, pl.ds(0, N - 1)], d_ss.at[gi])

    def send_groups(m, start, stop):
        def go(g, _):
            stage(m, g)
            launch(m * NG + g, peers)
            return 0

        lax.fori_loop(start, stop, go, 0)

    def exchange(m, start, back_m, back_start):
        def go(i, _):
            stage(m, start + i)
            drain(back_m * NG + back_start + i)
            launch(m * NG + start + i, peers)
            receive(back_m, back_start + i)
            return 0

        lax.fori_loop(0, 2, go, 0)

    def routers_out():
        wait_bytes(rt_r.at[pl.ds(0, N - 1)], rt_rs)
        for t in range(16):
            a, b = rt_r[2 * t].astype(F32), rt_r[2 * t + 1].astype(F32)
            top = jnp.concatenate([a[:, :64], b[:, :64]], axis=1)
            bot = jnp.concatenate([a[:, 64:], b[:, 64:]], axis=1)
            rt_x[e_id, :, pl.ds(128 * t, 128)] = jnp.concatenate([top, bot], axis=0).astype(BF16)
        hop(rt_x.at[e_id], rx_ss.at[0], rx_rs.at[0], partner).start()
        hop(rt_x.at[e_id, :, pl.ds(0, 1024)], rx_ss.at[1], rx_rs.at[1], right).start()
        hop(rt_x.at[e_id, :, pl.ds(1024, 1024)], rx_ss.at[2], rx_rs.at[2], left).start()

    merge(0, 0)
    stage(0, 0)
    pl.semaphore_wait(barrier, len(peers) + len(mates))
    launch(0, peers)
    merge(0, 1)
    start_rs(0)
    send_groups(0, 1, 2)
    merge(1, 0)
    start_rs(1)
    send_groups(0, 2, 3)
    merge(2, 0)
    start_rs(2)
    for c in router_in:
        c.wait()
    rt = rwb[...] * rgb[...]
    rt_s[...] = jnp.concatenate([rt[:8], rt[8:]], axis=1).astype(BF16)
    send_all(lambda p: rt_s, rt_r.at[me], rt_ss, rt_rs)
    rt_r[me] = rt_s[...]
    send_groups(0, 3, NG)
    if AHEAD > NG:
        send_groups(1, 0, AHEAD - NG)
    finish_rs(0)
    for back in range(0, 3 * NG - AHEAD, 2):
        bm, bg = divmod(back, NG)
        m, g = divmod(back + AHEAD, NG)
        if bg == 0 and bm:
            finish_rs(bm)
        exchange(m, g, bm, bg)
        if back == 0:
            routers_out()
        if back == 2:
            wait_bytes(rt_x.at[0, :, pl.ds(0, 1024)], rx_rs.at[1])
            wait_bytes(rt_x.at[0, :, pl.ds(0, 1024)], rx_rs.at[2])
            hop(rt_x.at[other], rx_ss.at[3], rx_rs.at[3], partner).start()
    wait_bytes(rt_x.at[0], rx_rs.at[0])
    wait_bytes(rt_x.at[0], rx_rs.at[3])
    for k in range(4):
        orr[pl.ds(16 * k, 16), :] = rt_x[k]
    for back in range(3 * NG - AHEAD, 3 * NG, 2):
        bm, bg = divmod(back, NG)
        if bg == 0:
            finish_rs(bm)

        def come(i, _):
            receive(bm, bg + i)
            return 0

        lax.fori_loop(0, 1 if back + 2 == 3 * NG else 2, come, 0)
    wait_bytes(rcv.at[3 * NG - 1, pl.ds(0, N - 1)], d_rs.at[3 * NG - 1])
    last[...] = rcv[3 * NG - 1]
    lfac[...] = fac[NG - 1]
    wait_bytes(rt_x.at[0], rx_ss.at[0])
    wait_bytes(rt_x.at[0, :, pl.ds(0, 1024)], rx_ss.at[1])
    wait_bytes(rt_x.at[0, :, pl.ds(0, 1024)], rx_ss.at[2])
    wait_bytes(rt_x.at[0], rx_ss.at[3])
    wait_bytes(rt_r.at[pl.ds(0, N - 1)], rt_ss)
    for m in range(3):
        wait_bytes(rs_r.at[m, pl.ds(0, N - 1)], rs_ss.at[m])

    def drained(gi, _):
        drain(gi)
        return 0

    lax.fori_loop(3 * NG - AHEAD, 3 * NG, drained, 0)


def put_out(og, ou, od, cg, cu, cd, orr, last, lfac, hg, hu, hd, hcg, hcu, hcd, hr, tail, sem):
    done = pl.ds(0, E - GE)
    rest = pl.ds(E - GE, GE)
    pairs = ((og, hg), (ou, hu), (od.at[done], hd.at[done]), (cg, hcg), (cu, hcu), (cd, hcd), (orr, hr))
    copies = [pltpu.make_async_copy(a, b, sem.at[i]) for i, (a, b) in enumerate(pairs)]
    for c in copies:
        c.start()

    for t in range(N // 2):
        for i, x in enumerate(decoded(t, last, lfac)):
            tail[i, :, pl.ds(128 * t, 128)] = x
    copies.append(pltpu.make_async_copy(tail, hd.at[rest], sem.at[7]))
    copies[-1].start()
    for c in copies:
        c.wait()


def per_device(
    master_gate, second_gate, master_up, second_up, master_down, second_down, router_weight, router_gain
):
    vmem = pl.BlockSpec(memory_space=pltpu.VMEM)
    hbm = pl.BlockSpec(memory_space=pltpu.HBM)
    dma = pltpu.SemaphoreType.DMA
    big = jax.ShapeDtypeStruct((E, W, N * R), BF16)
    small = jax.ShapeDtypeStruct((E, W), F32)
    raw = (jax.ShapeDtypeStruct((N, GE // 2, W, 128), BF16), jax.ShapeDtypeStruct((GE, W, 128), F32))
    shapes = (big, big, big, small, small, small, jax.ShapeDtypeStruct((4 * E, N * R), BF16))
    results = pl.pallas_call(
        kernel,
        out_shape=shapes + raw,
        in_specs=[hbm] * 8,
        out_specs=(vmem,) * 9,
        scratch_shapes=[
            pltpu.VMEM((16, R), F32),
            pltpu.VMEM((1, R), F32),
            pltpu.VMEM((3, E, R, C), F32),
            pltpu.VMEM((3, E, R, C), BF16),
            pltpu.VMEM((3, GE, NG, C), F32),
            pltpu.VMEM((3, E, 1, C), F32),
            pltpu.VMEM((NG, GE, W, 128), F32),
            pltpu.VMEM((3, N, NG, 128), F32),
            pltpu.VMEM((3, N, NG, 128), F32),
            pltpu.VMEM((3 * NG, N, GE // 2, W, 128), BF16),
            pltpu.VMEM((3 * NG, N, GE // 2, W, 128), BF16),
            pltpu.VMEM((8, 128), BF16),
            pltpu.VMEM((N, 8, 128), BF16),
            pltpu.VMEM((4, 16, N * R), BF16),
            dma((2, 3 * NG)), dma((2,)), dma((3,)), dma((3,)), pltpu.SemaphoreType.REGULAR, dma((3 * NG,)), dma((3 * NG,)),
            dma, dma, dma((4,)), dma((4,)),
        ],
        compiler_params=pltpu.CompilerParams(
            collective_id=0, has_side_effects=True, vmem_limit_bytes=44 * 2**20
        ),
        name="reshard",
    )(
        *(
            pltpu.with_memory_space_constraint(x, pltpu.HBM)
            for x in (
                master_gate, second_gate, master_up, second_up,
                jnp.swapaxes(master_down, 1, 2), jnp.swapaxes(second_down, 1, 2),
                router_weight.T, router_gain[None, :],
            )
        )
    )
    gate, up, down, cg, cu, cd, router = pl.pallas_call(
        put_out,
        out_shape=shapes,
        in_specs=[vmem] * 9,
        out_specs=(hbm,) * 7,
        scratch_shapes=[pltpu.VMEM((GE, W, N * R), BF16), dma((8,))],
        compiler_params=pltpu.CompilerParams(vmem_limit_bytes=4 * 2**20),
        name="put_out",
    )(*results)
    return (jnp.swapaxes(gate, 1, 2), jnp.swapaxes(up, 1, 2), down, cg, cu, cd, router.T)


def solution(mesh):
    wide, tall = P("expert", "shard", None), P("expert", None, "shard")
    return jax.shard_map(
        per_device,
        mesh=mesh,
        in_specs=(wide, wide, wide, wide, tall, tall, P("shard", "expert"), P("shard")),
        out_specs=(tall, tall, wide, P("expert", "shard"), P("expert", "shard"), P("expert", "shard"), P()),
        check_vma=False,
    )
```

time: 88.8 us -> 86.5 us (0.974)
  Pallas kernels: 88 us -> 85.1 us
    pallas_call x2, Pallas kernels: 88 us -> 85.1 us  [the longest x1 82.3 us: per_device(): pl.pallas_call(kernel, out_shape=shapes + raw, in_specs=[hbm] * 8, out_sp...]
where the time goes in v4:
time: 86.5 us; the launch traced here: 85.7 us
  Pallas kernels  85.1 us (98%)
    pallas_call x1, Pallas kernels, per_device(): pl.pallas_call(kernel, out_shape=shapes + raw, in_specs=[hbm] * 8, out_sp...  82.3 us
    pallas_call x1, Pallas kernels, per_device(): pl.pallas_call(put_out, out_shape=shapes, in_specs=[vmem] * 9, out_specs=...  2.81 us

profile of v4, /device:TPU:0, one launch (start us, length us, event | category | flops | bytes accessed | tf_op | source)
XLA Modules:
  0.0 85.7 jit_solution(962816344410194676)
XLA Ops:
  0.6 82.3 %reshard.1 = (bf16[16,32,2048]{2,1,0:T(8,128)(2,1)S(1)}, bf16[16,32,2048]{2,1,0:T(8,128)(2,1)S(1)}, bf16[16,32,2048]{2,1,0:T(8,128)(2,1)S(1)}, f32[16,32]{1,0:T(...) custom-call(f32[16,64,1024]{2,1,0:T(8,128)} %mg.1, ...), custom_call_target="tpu_custom_call" | custom-call | tf_op jit(solution)/shard_map/reshard/pallas_call | solution.py:314
  82.9 2.8 %put_out.1 = (bf16[16,32,2048]{2,1,0:T(8,128)(2,1)}, bf16[16,32,2048]{2,1,0:T(8,128)(2,1)}, bf16[16,32,2048]{2,1,0:T(8,128)(2,1)}, f32[16,32]{1,0:T(8,128)}, f32...) custom-call(bf16[16,32,2048]{2,1,0:T(8,128)(2,1)S(1)} %get-tuple-element.23.og, ...), custom_call_target="tpu_custom_call" | custom-call | tf_op jit(solution)/shard_map/put_out/pallas_call | solution.py:351

commit v5 on v4

--- a/solution.py
+++ b/solution.py
@@ -24,8 +24,7 @@
 
 OFFSETS = sorted(
     [(dx, dy, dz) for dx in range(2) for dy in range(4) for dz in range(4) if (dx, dy, dz) != (0, 0, 0)],
-    key=hops,
-    reverse=True,
+    key=lambda o: (-hops(o), (o[1] + 2 * o[2]) % 4, o[0]),
 )
 AHEAD = 4
 FAR = sum(hops(o) > 3 for o in OFFSETS)
@@ -56,7 +55,7 @@
     mg, sg, mu, su, md, sd, rw, rg,
     og, ou, od, cg, cu, cd, orr, last, lfac,
     rwb, rgb, mbuf, sbuf, lmax, inl, fac, rs_s, rs_r, snd, rcv, rt_s, rt_r, rt_x,
-    load_sem, rt_ld, rs_ss, rs_rs, ready, d_ss, d_rs, rt_ss, rt_rs, rx_ss, rx_rs,
+    load_sem, rt_ld, rs_ss, rs_rs, d_ss, d_rs, rt_ss, rt_rs, rx_ss, rx_rs,
 ):
     e_id = lax.axis_index("expert")
     me = lax.axis_index("shard")
@@ -266,9 +265,6 @@
             return 0
 
         lax.fori_loop(0, 1 if back + 2 == 3 * NG else 2, come, 0)
-    wait_bytes(rcv.at[3 * NG - 1, pl.ds(0, N - 1)], d_rs.at[3 * NG - 1])
-    last[...] = rcv[3 * NG - 1]
-    lfac[...] = fac[NG - 1]
     wait_bytes(rt_x.at[0], rx_ss.at[0])
     wait_bytes(rt_x.at[0, :, pl.ds(0, 1024)], rx_ss.at[1])
     wait_bytes(rt_x.at[0, :, pl.ds(0, 1024)], rx_ss.at[2])
@@ -282,6 +278,9 @@
         return 0
 
     lax.fori_loop(3 * NG - AHEAD, 3 * NG, drained, 0)
+    wait_bytes(rcv.at[3 * NG - 1, pl.ds(0, N - 1)], d_rs.at[3 * NG - 1])
+    last[...] = rcv[3 * NG - 1]
+    lfac[...] = fac[NG - 1]
 
 
 def put_out(og, ou, od, cg, cu, cd, orr, last, lfac, hg, hu, hd, hcg, hcu, hcd, hr, tail, sem):
@@ -331,7 +330,7 @@
             pltpu.VMEM((8, 128), BF16),
             pltpu.VMEM((N, 8, 128), BF16),
             pltpu.VMEM((4, 16, N * R), BF16),
-            dma((2, 3 * NG)), dma((2,)), dma((3,)), dma((3,)), pltpu.SemaphoreType.REGULAR, dma((3 * NG,)), dma((3 * NG,)),
+            dma((2, 3 * NG)), dma((2,)), dma((3,)), dma((3,)), dma((3 * NG,)), dma((3 * NG,)),
             dma, dma, dma((4,)), dma((4,)),
         ],
         compiler_params=pltpu.CompilerParams(

time: 86.5 us -> 85.9 us (level)
  no operation moved by 1% of the time
where the time goes in v5:
time: 85.9 us; the launch traced here: 85.8 us
  Pallas kernels  85.1 us (99%)
    pallas_call x1, Pallas kernels, per_device(): pl.pallas_call(kernel, out_shape=shapes + raw, in_specs=[hbm] * 8, out_sp...  82.3 us
    pallas_call x1, Pallas kernels, per_device(): pl.pallas_call(put_out, out_shape=shapes, in_specs=[vmem] * 9, out_specs=...  2.81 us

profile of v5, /device:TPU:0, one launch (start us, length us, event | category | flops | bytes accessed | tf_op | source)
XLA Modules:
  0.0 85.8 jit_solution(13084906379821347191)
XLA Ops:
  0.6 82.3 %reshard.1 = (bf16[16,32,2048]{2,1,0:T(8,128)(2,1)S(1)}, bf16[16,32,2048]{2,1,0:T(8,128)(2,1)S(1)}, bf16[16,32,2048]{2,1,0:T(8,128)(2,1)S(1)}, f32[16,32]{1,0:T(...) custom-call(f32[16,64,1024]{2,1,0:T(8,128)} %mg.1, ...), custom_call_target="tpu_custom_call" | custom-call | tf_op jit(solution)/shard_map/reshard/pallas_call | solution.py:313
  82.9 2.8 %put_out.1 = (bf16[16,32,2048]{2,1,0:T(8,128)(2,1)}, bf16[16,32,2048]{2,1,0:T(8,128)(2,1)}, bf16[16,32,2048]{2,1,0:T(8,128)(2,1)}, f32[16,32]{1,0:T(8,128)}, f32...) custom-call(bf16[16,32,2048]{2,1,0:T(8,128)(2,1)S(1)} %get-tuple-element.23.og, ...), custom_call_target="tpu_custom_call" | custom-call | tf_op jit(solution)/shard_map/put_out/pallas_call | solution.py:350

commit v6 on v5

--- a/solution.py
+++ b/solution.py
@@ -26,7 +26,7 @@
     [(dx, dy, dz) for dx in range(2) for dy in range(4) for dz in range(4) if (dx, dy, dz) != (0, 0, 0)],
     key=lambda o: (-hops(o), (o[1] + 2 * o[2]) % 4, o[0]),
 )
-AHEAD = 4
+AHEAD = 6
 FAR = sum(hops(o) > 3 for o in OFFSETS)
 
 

time: 85.9 us -> 85.9 us (level)
  no operation moved by 1% of the time
where the time goes in v6:
time: 85.9 us; the launch traced here: 85.8 us
  Pallas kernels  85.1 us (99%)
    pallas_call x1, Pallas kernels, per_device(): pl.pallas_call(kernel, out_shape=shapes + raw, in_specs=[hbm] * 8, out_sp...  82.3 us
    pallas_call x1, Pallas kernels, per_device(): pl.pallas_call(put_out, out_shape=shapes, in_specs=[vmem] * 9, out_specs=...  2.81 us

profile of v6, /device:TPU:0, one launch (start us, length us, event | category | flops | bytes accessed | tf_op | source)
XLA Modules:
  0.0 85.8 jit_solution(17338515887945940112)
XLA Ops:
  0.6 82.3 %reshard.1 = (bf16[16,32,2048]{2,1,0:T(8,128)(2,1)S(1)}, bf16[16,32,2048]{2,1,0:T(8,128)(2,1)S(1)}, bf16[16,32,2048]{2,1,0:T(8,128)(2,1)S(1)}, f32[16,32]{1,0:T(...) custom-call(f32[16,64,1024]{2,1,0:T(8,128)} %mg.1, ...), custom_call_target="tpu_custom_call" | custom-call | tf_op jit(solution)/shard_map/reshard/pallas_call | solution.py:313
  82.9 2.8 %put_out.1 = (bf16[16,32,2048]{2,1,0:T(8,128)(2,1)}, bf16[16,32,2048]{2,1,0:T(8,128)(2,1)}, bf16[16,32,2048]{2,1,0:T(8,128)(2,1)}, f32[16,32]{1,0:T(8,128)}, f32...) custom-call(bf16[16,32,2048]{2,1,0:T(8,128)(2,1)S(1)} %get-tuple-element.23.og, ...), custom_call_target="tpu_custom_call" | custom-call | tf_op jit(solution)/shard_map/put_out/pallas_call | solution.py:350
